TPU v7x, 128 devices: a whole 4x4x4 slice. The times are simulated.
128 devices in a mesh: series: 16 (over z, x), tm: 8 (over y, core).
Axes of the slice: x: 4, y: 4, z: 4, core: 2. Of those that a mesh axis runs over, the one named last changes fastest.
Arguments:
- data: bfloat16 [65536, 4096], P('series', 'tm'), may hold values from -24 to 24
- factors_init: bfloat16 [4096, 256], P('tm'), may hold values from -6 to 6
Outputs:
- loadings: bfloat16 [65536, 256], P('series')
- factors: bfloat16 [4096, 256], P('tm')
- innovations: float32 [4096, 256], P('tm')
- transition: float32 [256, 256], replicated
- residual_share: float32 [], replicated
All inputs are finite; a program needn't handle non-finite values.
Results may differ from a plain program's by a relative error of at most 0.015.
Values may be sent and summed in bfloat16 or wider, within the bound.
A program may use at most 128 MiB of HBM per device.

v0:
```python
import jax
import jax.numpy as jnp
from jax import lax
from jax.experimental import pallas as pl
from jax.experimental.pallas import tpu as pltpu
from jax.sharding import PartitionSpec as P

ITERS = 3


RIDGE = 0.01


def sent_to_all(shard, axis):
    copies = jnp.broadcast_to(shard, (lax.axis_size(axis), *shard.shape))
    return lax.all_to_all(copies, axis, split_axis=0, concat_axis=0, tiled=True)


def taken_together(shard, axis):
    everything = sent_to_all(shard, axis)
    return jnp.sum(everything, axis=0)


def packed_total(arrays, axis):
    ends = [0]
    for a in arrays:
        ends.append(ends[-1] + a.size)
    running = taken_together(jnp.concatenate([a.ravel() for a in arrays]), axis)
    return tuple((running[b:e].reshape(a.shape) for a, b, e in zip(arrays, ends, ends[1:])))


def in_blocks(shard, dim, length):
    dims = shard.shape
    tiles = shard.reshape(*dims[:dim], length, dims[dim] // length, *dims[dim + 1 :])
    return jnp.moveaxis(tiles, dim, 0)


def sum_at_owner(shard, axis, dim):
    tiles = in_blocks(shard, dim, lax.axis_size(axis))
    arrived = lax.all_to_all(tiles, axis, split_axis=0, concat_axis=0, tiled=True)
    return arrived.sum(axis=0)


def laid_out(tiles, dim):
    dims = list(tiles.shape[1:])
    dims[dim] *= tiles.shape[0]
    return jnp.moveaxis(tiles, 0, dim).reshape(dims)


def collect(shard, axis, dim):
    tiles = sent_to_all(shard, axis)
    return laid_out(tiles, dim)


def passed_along(block, axis, distance):
    devices = range(lax.axis_size(axis))
    route = [(i - distance, i) for i in devices if i - distance in devices]
    return lax.ppermute(block, axis, route)


def in_one(arrays, axis):
    ravelled, at, gathered = (jnp.concatenate([a.reshape(-1) for a in arrays]), 0, [])
    running = lax.psum(ravelled, axis)
    for a in arrays:
        gathered.append(running[at : at + a.size].reshape(a.shape))
        at += a.size
    return tuple(gathered)


def inverse_kernel(g_ref, out_ref, a_ref, x_ref, e_ref):
    n = g_ref.shape[0]
    rows = lax.broadcasted_iota(jnp.int32, (n, n), 0)
    cols = lax.broadcasted_iota(jnp.int32, (n, n), 1)
    diagonal = rows == cols
    gram = g_ref[...] + jnp.where(diagonal, RIDGE, 0.0)
    masked = jnp.where(diagonal, gram, 0.0)
    down = lax.rsqrt(jnp.sum(masked, axis=1, keepdims=True))
    across = lax.rsqrt(jnp.sum(masked, axis=0, keepdims=True))
    scaled = gram * down * across
    a_ref[...] = scaled
    bound = jnp.max(jnp.sum(jnp.abs(scaled), axis=0, keepdims=True))
    alpha = 1.9 / bound
    start = jnp.where(diagonal, alpha, 0.0)
    x_ref[...] = start
    e_ref[...] = jnp.where(diagonal, 1.0, 0.0) - alpha * scaled

    def narrow(left, right):
        return jnp.dot(
            left.astype(jnp.bfloat16),
            right.astype(jnp.bfloat16),
            preferred_element_type=jnp.float32,
        )

    def wide(left, right):
        return jnp.dot(
            left, right, precision=lax.Precision.HIGHEST, preferred_element_type=jnp.float32
        )

    def squaring(carry):
        step, _ = carry
        for _ in range(2):
            error = e_ref[...]
            guess = x_ref[...]
            e_ref[...] = narrow(error, error)
            x_ref[...] = guess + narrow(guess, error)
        final = e_ref[...]
        return step + 1, jnp.sum(final * final)

    lax.while_loop(
        lambda c: jnp.logical_and(c[0] < 10, jnp.logical_and(c[1] > 1e-2, c[1] < 1e3)),
        squaring,
        (0, jnp.float32(1.0)),
    )

    def residual():
        error = jnp.where(diagonal, 1.0, 0.0) - wide(a_ref[...], x_ref[...])
        e_ref[...] = error
        return jnp.max(jnp.abs(error))

    def refine(carry):
        step, _ = carry
        worst = residual()
        guess = x_ref[...]
        x_ref[...] = guess + narrow(guess, e_ref[...])
        return step + 1, worst

    _, worst = lax.while_loop(
        lambda c: jnp.logical_and(c[0] < 8, jnp.logical_and(c[1] >= 5e-4, c[1] < 2.0)),
        refine,
        (0, jnp.float32(1.0)),
    )

    @pl.when(worst >= 5e-4)
    def _():
        x_ref[...] = jnp.where(diagonal, alpha, 0.0)

        def newton(carry):
            step, _ = carry
            error = residual()
            guess = x_ref[...]
            x_ref[...] = guess + wide(guess, e_ref[...])
            return step + 1, error

        lax.while_loop(
            lambda c: jnp.logical_and(c[0] < 48, c[1] >= 5e-4),
            newton,
            (0, jnp.float32(1.0)),
        )

    out_ref[...] = x_ref[...] * down * across


def regularized_inverse(gram):
    n = gram.shape[0]
    square = pltpu.VMEM((n, n), jnp.float32)
    return pl.pallas_call(
        inverse_kernel,
        out_shape=jax.ShapeDtypeStruct((n, n), jnp.float32),
        in_specs=[pl.BlockSpec(memory_space=pltpu.VMEM)],
        out_specs=pl.BlockSpec(memory_space=pltpu.VMEM),
        scratch_shapes=[square] * 3,
        compiler_params=pltpu.CompilerParams(vmem_limit_bytes=16 * 1024 * 1024),
        name="inverse",
    )(gram)


def column_gram(left, right):
    return lax.dot_general(
        left, right, (((0,), (0,)), ((), ())), preferred_element_type=jnp.float32
    )


def body(data, factors_init):
    precise = lax.Precision.HIGHEST
    factors = factors_init
    data_squares = jnp.sum(jnp.square(data.astype(jnp.float32)))
    loadings = None
    cross = None
    gram_loadings = None
    data_total = None
    for sweep_index in range(ITERS):
        gram_part = column_gram(factors, factors)
        gram_factors, data_block = packed_total((gram_part, data_squares), "tm")
        current = factors
        projection = sum_at_owner(
            jnp.dot(data, current, preferred_element_type=jnp.float32), "tm", 0
        )
        loading_share = jnp.dot(
            projection, regularized_inverse(gram_factors), precision=precise
        ).astype(jnp.bfloat16)
        loadings = collect(loading_share, "tm", 0)
        loading_part = column_gram(loadings, loadings)
        cross_part = column_gram(data, loadings)
        gram_loadings, cross, data_total = lax.psum(
            (loading_part, cross_part, data_block), "series"
        )
        factors = jnp.dot(cross, regularized_inverse(gram_loadings), precision=precise).astype(
            jnp.bfloat16
        )
    previous = passed_along(factors[-1:], "tm", 1)
    earlier = jnp.concatenate([previous, factors[:-1]], axis=0)
    lagged_part = column_gram(factors, earlier)
    base_part = column_gram(earlier, earlier)
    own_gram = column_gram(factors, factors)
    factors_wide = factors.astype(jnp.float32)
    scalar_part = jnp.sum(gram_loadings * own_gram) - 2.0 * jnp.sum(factors_wide * cross)
    lagged, base_gram, expanded = in_one((lagged_part, base_part, scalar_part), "tm")
    residual_total = data_total + expanded
    transition = jnp.dot(lagged, regularized_inverse(base_gram), precision=precise)
    predicted = lax.dot_general(
        earlier.astype(jnp.float32),
        transition,
        (((1,), (1,)), ((), ())),
        precision=precise,
        preferred_element_type=jnp.float32,
    )
    innovations = factors.astype(jnp.float32) - predicted
    residual_share = residual_total / data_total
    return (loadings, factors, innovations, transition, residual_share)


def solution(mesh):
    return jax.shard_map(
        body,
        mesh=mesh,
        in_specs=(P("series", "tm"), P("tm", None)),
        out_specs=(P("series", None), P("tm", None), P("tm", None), P(), P()),
        check_vma=False,
    )
```

profile of v0, /device:TPU:1, one launch (start us, length us, event | category | flops | bytes accessed | tf_op | source)
XLA Modules:
  0.0 762.1 jit_solution(15327552027347245243)
XLA Ops:
  15.7 6.0 all-to-all-start.1
  21.6 5.4 fusion.6
  27.0 20.9 %all-to-all-done.1 = f32[8,1,65537]{2,1,0:T(1,128)S(1)} async-done(((f32[8,1,65537]{2,1,0:T(1,128)}), f32[8,1,65537]{2,1,0:T(1,128)S(1)}, u32[]{:S(2)}, u32[]{:S(2)}) %all-to-all-start.1) | async-done | bytes 2097216 | tf_op jit(solution)/shard_map/all_to_all | solution.py:16
  47.9 5.4 all-to-all-start
  59.3 42.8 %all-to-all-done = f32[8,512,256]{2,1,0:T(8,128)} async-done(((f32[8,512,256]{2,1,0:T(8,128)}), f32[8,512,256]{2,1,0:T(8,128)}, u32[]{:S(2)}, u32[]{:S(2)}) %all-to-all-start) | async-done | bytes 4194336 | tf_op jit(solution)/shard_map/all_to_all | solution.py:40
  105.3 29.8 %all_to_all.48 = bf16[8,512,256]{2,1,0:T(8,128)(2,1)S(1)} all-to-all(bf16[8,512,256]{2,1,0:T(8,128)(2,1)S(1)} %broadcast_in_dim.19), channel_id=1, replica_groups=mesh['series'=16,'tm'=8] {'tm'}, dimensions={0} | all-to-all | bytes 4194304 | tf_op jit(solution)/shard_map/all_to_all | solution.py:16
  138.7 86.2 %all-reduce.14.cloned.1.call-done = (f32[512,256]{0,1:T(8,128)}, f32[256,256]{1,0:T(8,128)}) async-done(((f32[512,256]{0,1:T(8,128)}, f32[256,256]{1,0:T(8,128)}), (f32[512,256]{0,1:T(8,128)}, f32[256,256]{1,0:T(8,128)})) %all-reduce.14.cloned.1.call-update) | async-done | bytes 786448 | tf_op jit(solution)/shard_map/psum | solution.py:194
  225.9 6.3 inverse.8
  237.7 6.4 all-to-all-start.4
  250.2 20.2 %all-to-all-done.4 = f32[8,1,65537]{2,1,0:T(1,128)S(1)} async-done(((f32[8,1,65537]{2,1,0:T(1,128)}), f32[8,1,65537]{2,1,0:T(1,128)S(1)}, u32[]{:S(2)}, u32[]{:S(2)}) %all-to-all-start.4) | async-done | bytes 2097216 | tf_op jit(solution)/shard_map/all_to_all | solution.py:16
  270.4 5.4 all-to-all-start.3
  281.8 42.8 %all-to-all-done.3 = f32[8,512,256]{1,2,0:T(8,128)} async-done(((f32[8,512,256]{1,2,0:T(8,128)}), f32[8,512,256]{1,2,0:T(8,128)}, u32[]{:S(2)}, u32[]{:S(2)}) %all-to-all-start.3) | async-done | bytes 4194336 | tf_op jit(solution)/shard_map/all_to_all | solution.py:40
  328.5 30.1 %all_to_all.49 = bf16[8,512,256]{2,1,0:T(8,128)(2,1)S(1)} all-to-all(bf16[8,512,256]{2,1,0:T(8,128)(2,1)S(1)} %broadcast_in_dim.21), channel_id=1, replica_groups=mesh['series'=16,'tm'=8] {'tm'}, dimensions={0} | all-to-all | bytes 4194304 | tf_op jit(solution)/shard_map/all_to_all | solution.py:16
  362.1 83.2 %all-reduce.12.cloned.1.call-done = (f32[512,256]{0,1:T(8,128)}, f32[256,256]{1,0:T(8,128)}) async-done(((f32[512,256]{0,1:T(8,128)}, f32[256,256]{1,0:T(8,128)}), (f32[512,256]{0,1:T(8,128)}, f32[256,256]{1,0:T(8,128)})) %all-reduce.12.cloned.1.call-update) | async-done | bytes 786448 | tf_op jit(solution)/shard_map/psum | solution.py:194
  446.2 6.2 inverse.10
  457.9 6.4 all-to-all-start.7
  470.4 20.2 %all-to-all-done.7 = f32[8,1,65537]{2,1,0:T(1,128)S(1)} async-done(((f32[8,1,65537]{2,1,0:T(1,128)}), f32[8,1,65537]{2,1,0:T(1,128)S(1)}, u32[]{:S(2)}, u32[]{:S(2)}) %all-to-all-start.7) | async-done | bytes 2097216 | tf_op jit(solution)/shard_map/all_to_all | solution.py:16
  490.6 5.4 all-to-all-start.6
  502.2 42.5 %all-to-all-done.6 = f32[8,512,256]{1,2,0:T(8,128)} async-done(((f32[8,512,256]{1,2,0:T(8,128)}), f32[8,512,256]{1,2,0:T(8,128)}, u32[]{:S(2)}, u32[]{:S(2)}) %all-to-all-start.6) | async-done | bytes 4194336 | tf_op jit(solution)/shard_map/all_to_all | solution.py:40
  548.6 29.8 %all_to_all.50 = bf16[8,512,256]{2,1,0:T(8,128)(2,1)S(1)} all-to-all(bf16[8,512,256]{2,1,0:T(8,128)(2,1)S(1)} %broadcast_in_dim.23), channel_id=1, replica_groups=mesh['series'=16,'tm'=8] {'tm'}, dimensions={0} | all-to-all | bytes 4194304 | tf_op jit(solution)/shard_map/all_to_all | solution.py:16
  582.1 83.1 %all-reduce.10.cloned.1.call-done = (f32[512,256]{0,1:T(8,128)}, f32[256,256]{1,0:T(8,128)}) async-done(((f32[512,256]{0,1:T(8,128)}, f32[256,256]{1,0:T(8,128)}), (f32[512,256]{0,1:T(8,128)}, f32[256,256]{1,0:T(8,128)})) %all-reduce.10.cloned.1.call-update) | async-done | bytes 786448 | tf_op jit(solution)/shard_map/psum | solution.py:194
  666.1 6.1 inverse.12
  684.6 31.5 %psum.63 = f32[]{:T(128)} all-reduce(f32[]{:T(128)} %bitcast.14), channel_id=1, replica_groups=mesh['series'=16,'tm'=8] {'series'}, use_global_device_ids=true, to_apply=%region_16.0 | all-reduce | flops 1 | bytes 8 | tf_op jit(solution)/shard_map/psum | solution.py:194
  716.9 25.1 %all-reduce.8.cloned.1.call-done = f32[131073]{0:T(1024)} async-done(((f32[131073]{0:T(1024)}), f32[131073]{0:T(1024)}) %all-reduce.8.cloned.1.call-update) | async-done | bytes 524308 | tf_op jit(solution)/shard_map/psum | solution.py:63
  (93 shorter events, 96.0 us)
Async XLA Ops:
  7.2 5.0 copy-start
  15.7 32.2 %all-to-all-start.1 = ((f32[8,1,65537]{2,1,0:T(1,128)}), f32[8,1,65537]{2,1,0:T(1,128)S(1)}, u32[]{:S(2)}, u32[]{:S(2)}) async-start(f32[8,1,65537]{2,1,0:T(1,128)} %broadcast_in_dim.18), calls=%async_computation.1 | async-start | bytes 4202496 | tf_op jit(solution)/shard_map/all_to_all | solution.py:16
  47.9 54.2 %all-to-all-start = ((f32[8,512,256]{2,1,0:T(8,128)}), f32[8,512,256]{2,1,0:T(8,128)}, u32[]{:S(2)}, u32[]{:S(2)}) async-start(f32[8,512,256]{2,1,0:T(8,128)} %bitcast.88), calls=%async_computation | async-start | bytes 8388608 | tf_op jit(solution)/shard_map/all_to_all | solution.py:40
  53.3 171.6 %all-reduce.14.cloned.1.call-start = ((), (), s32[]{:S(2)}) async-start(), calls=%async_computation.12 | async-start | bytes 1572864 | tf_op jit(solution)/shard_map/psum | solution.py:194
  105.3 29.9 %copy-start.5 = (bf16[4096,512]{1,0:T(8,128)(2,1)S(1)}, bf16[4096,512]{1,0:T(8,128)(2,1)}, u32[]{:S(2)}) copy-start(bf16[4096,512]{1,0:T(8,128)(2,1)} %param.2) | copy-start | bytes 12582916
  224.9 0.9 copy-start.3
  237.7 32.7 %all-to-all-start.4 = ((f32[8,1,65537]{2,1,0:T(1,128)}), f32[8,1,65537]{2,1,0:T(1,128)S(1)}, u32[]{:S(2)}, u32[]{:S(2)}) async-start(f32[8,1,65537]{2,1,0:T(1,128)} %broadcast_in_dim.20), calls=%async_computation.4 | async-start | bytes 4202496 | tf_op jit(solution)/shard_map/all_to_all | solution.py:16
  270.4 54.2 %all-to-all-start.3 = ((f32[8,512,256]{1,2,0:T(8,128)}), f32[8,512,256]{1,2,0:T(8,128)}, u32[]{:S(2)}, u32[]{:S(2)}) async-start(f32[8,512,256]{1,2,0:T(8,128)} %bitcast.92), calls=%async_computation.3 | async-start | bytes 8388608 | tf_op jit(solution)/shard_map/all_to_all | solution.py:40
  275.8 169.4 %all-reduce.12.cloned.1.call-start = ((), (), s32[]{:S(2)}) async-start(), calls=%async_computation.11 | async-start | bytes 1572864 | tf_op jit(solution)/shard_map/psum | solution.py:194
  328.5 30.1 %copy-start.6 = (bf16[4096,512]{1,0:T(8,128)(2,1)S(1)}, bf16[4096,512]{1,0:T(8,128)(2,1)}, u32[]{:S(2)}) copy-start(bf16[4096,512]{1,0:T(8,128)(2,1)} %param.2) | copy-start | bytes 12582916
  445.2 0.9 copy-start.4
  457.9 32.7 %all-to-all-start.7 = ((f32[8,1,65537]{2,1,0:T(1,128)}), f32[8,1,65537]{2,1,0:T(1,128)S(1)}, u32[]{:S(2)}, u32[]{:S(2)}) async-start(f32[8,1,65537]{2,1,0:T(1,128)} %broadcast_in_dim.22), calls=%async_computation.7 | async-start | bytes 4202496 | tf_op jit(solution)/shard_map/all_to_all | solution.py:16
  490.6 54.2 %all-to-all-start.6 = ((f32[8,512,256]{1,2,0:T(8,128)}), f32[8,512,256]{1,2,0:T(8,128)}, u32[]{:S(2)}, u32[]{:S(2)}) async-start(f32[8,512,256]{1,2,0:T(8,128)} %bitcast.93), calls=%async_computation.6 | async-start | bytes 8388608 | tf_op jit(solution)/shard_map/all_to_all | solution.py:40
  496.0 169.2 %all-reduce.10.cloned.1.call-start = ((), (), s32[]{:S(2)}) async-start(), calls=%async_computation.10 | async-start | bytes 1572864 | tf_op jit(solution)/shard_map/psum | solution.py:194
  548.6 29.9 %copy-start.7 = (bf16[4096,512]{1,0:T(8,128)(2,1)S(1)}, bf16[4096,512]{1,0:T(8,128)(2,1)}, u32[]{:S(2)}) copy-start(bf16[4096,512]{1,0:T(8,128)(2,1)} %param.2) | copy-start | bytes 12582916
  582.0 160.0 %all-reduce.8.cloned.1.call-start = ((), (), s32[]{:S(2)}) async-start(), calls=%async_computation.9 | async-start | bytes 1056768 | tf_op jit(solution)/shard_map/psum | solution.py:63
  665.2 0.9 copy-start.2
  674.9 7.3 collective-permute-start
  751.2 2.8 copy-start.8
  751.7 2.3 copy-start.1
Sparse Core Ops, SparseCore 0:
  138.8 86.0 all-reduce.13
  362.2 83.0 all-reduce.11
  582.1 83.0 all-reduce.9
  684.2 57.7 all-reduce.7
where the time goes:
time: 773 us; the launch traced here: 762 us
  waiting for transfers between devices  467 us (60%)
  blocking collectives  121 us (16%)
  starting transfers between devices  40.2 us (5%)
  Pallas kernels  36.4 us (5%)
  matrix products  35.3 us (5%)
  local copies, waits for them, and re-layouts  22.8 us (3%)
  other arithmetic  20.3 us (3%)
  between operations  19 us (2%)
    psum x3, waiting for transfers between devices, body(): lax.psum((loading_part, cross_part, data_block), 'series')  252 us
    all_to_all x3, waiting for transfers between devices, sum_at_owner(): lax.all_to_all(tiles, axis, split_axis=0, concat_axis=0, tiled=True)  128 us
    all_to_all x3, blocking collectives, sent_to_all(): return lax.all_to_all(copies, axis, split_axis=0, concat_axis=0, tiled=True)  89.7 us
    all_to_all x3, waiting for transfers between devices, sent_to_all(): return lax.all_to_all(copies, axis, split_axis=0, concat_axis=0, tiled=True)  61.2 us
    pallas_call x7, Pallas kernels, regularized_inverse(): pl.pallas_call(inverse_kernel, out_shape=jax.ShapeDtypeStruct((n, n), jnp...  36.4 us
    psum x1, blocking collectives, body(): lax.psum((loading_part, cross_part, data_block), 'series')  31.5 us
    psum x1, waiting for transfers between devices, in_one(): running = lax.psum(ravelled, axis)  25.1 us
    all_to_all x3, starting transfers between devices, sent_to_all(): return lax.all_to_all(copies, axis, split_axis=0, concat_axis=0, tiled=True)  18.8 us
  transfers between devices with their start and end apart: 11, of which 10 were waited for; matrix products, arithmetic and copies ran while one was open for 3% of the time, Pallas kernels for 2%

commit v1 on v0

v1 whole, which is shorter than its diff:
```python
import functools

import jax
import jax.numpy as jnp
from jax import lax
from jax.experimental import pallas as pl
from jax.experimental.pallas import tpu as pltpu
from jax.sharding import PartitionSpec as P

ITERS = 3
RIDGE = 0.01
MESH = pl.DeviceIdType.MESH
F32 = jnp.float32
BF16 = jnp.bfloat16
DMA = pltpu.SemaphoreType.DMA


def narrow(left, right):
    return jnp.dot(left.astype(BF16), right.astype(BF16), preferred_element_type=F32)


def wide(left, right):
    return jnp.dot(left, right, precision=lax.Precision.HIGHEST, preferred_element_type=F32)


def column_gram(left, right):
    return lax.dot_general(left, right, (((0,), (0,)), ((), ())), preferred_element_type=F32)


def inverse_of(g_ref, a_ref, x_ref, e_ref):
    n = g_ref.shape[0]
    rows = lax.broadcasted_iota(jnp.int32, (n, n), 0)
    cols = lax.broadcasted_iota(jnp.int32, (n, n), 1)
    diagonal = rows == cols
    gram = g_ref[...] + jnp.where(diagonal, RIDGE, 0.0)
    masked = jnp.where(diagonal, gram, 0.0)
    down = lax.rsqrt(jnp.sum(masked, axis=1, keepdims=True))
    across = lax.rsqrt(jnp.sum(masked, axis=0, keepdims=True))
    scaled = gram * down * across
    a_ref[...] = scaled
    bound = jnp.max(jnp.sum(jnp.abs(scaled), axis=0, keepdims=True))
    alpha = 1.9 / bound
    start = jnp.where(diagonal, alpha, 0.0)
    x_ref[...] = start
    e_ref[...] = jnp.where(diagonal, 1.0, 0.0) - alpha * scaled

    def squaring(carry):
        step, _ = carry
        for _ in range(2):
            error = e_ref[...]
            guess = x_ref[...]
            e_ref[...] = narrow(error, error)
            x_ref[...] = guess + narrow(guess, error)
        final = e_ref[...]
        return step + 1, jnp.sum(final * final)

    lax.while_loop(
        lambda c: jnp.logical_and(c[0] < 10, jnp.logical_and(c[1] > 1e-2, c[1] < 1e3)),
        squaring,
        (0, jnp.float32(1.0)),
    )

    def residual():
        error = jnp.where(diagonal, 1.0, 0.0) - wide(a_ref[...], x_ref[...])
        e_ref[...] = error
        return jnp.max(jnp.abs(error))

    def refine(carry):
        step, _ = carry
        worst = residual()
        guess = x_ref[...]
        x_ref[...] = guess + narrow(guess, e_ref[...])
        return step + 1, worst

    _, worst = lax.while_loop(
        lambda c: jnp.logical_and(c[0] < 8, jnp.logical_and(c[1] >= 5e-4, c[1] < 2.0)),
        refine,
        (0, jnp.float32(1.0)),
    )

    @pl.when(worst >= 5e-4)
    def _():
        x_ref[...] = jnp.where(diagonal, alpha, 0.0)

        def newton(carry):
            step, _ = carry
            error = residual()
            guess = x_ref[...]
            x_ref[...] = guess + wide(guess, e_ref[...])
            return step + 1, error

        lax.while_loop(
            lambda c: jnp.logical_and(c[0] < 48, c[1] >= 5e-4),
            newton,
            (0, jnp.float32(1.0)),
        )

    return x_ref[...] * down * across


def solve_kernel(g_ref, m_ref, out_ref, a_ref, x_ref, e_ref):
    inverse = inverse_of(g_ref, a_ref, x_ref, e_ref)
    out_ref[...] = wide(m_ref[...], inverse).astype(out_ref.dtype)


def in_vmem(count):
    return [pl.BlockSpec(memory_space=pltpu.VMEM)] * count


def solve(gram, rows):
    square = pltpu.VMEM(gram.shape, F32)
    return pl.pallas_call(
        solve_kernel,
        out_shape=jax.ShapeDtypeStruct(rows.shape, BF16),
        in_specs=in_vmem(2),
        out_specs=in_vmem(1)[0],
        scratch_shapes=[square] * 3,
        compiler_params=pltpu.CompilerParams(vmem_limit_bytes=16 * 1024 * 1024),
        name="solve",
    )(gram, rows)


class Place:
    def __init__(self):
        self.p = lax.axis_index("series")
        self.t = lax.axis_index("tm")
        self.planes = lax.axis_size("series")
        self.times = lax.axis_size("tm")
        self.ring = self.times // 2
        self.y = lax.div(self.t, 2)
        self.c = lax.rem(self.t, 2)
        self.partner = self.t + 1 - 2 * self.c

    def ring_at(self, distance):
        return lax.rem(self.y + distance, self.ring)

    def time_of(self, y):
        return 2 * y + self.c

    def copy(self, src, dst, send, recv, p=None, t=None):
        return pltpu.make_async_remote_copy(
            src_ref=src,
            dst_ref=dst,
            send_sem=send,
            recv_sem=recv,
            device_id=(self.p if p is None else p, self.t if t is None else t),
            device_id_type=MESH,
        )

    def greet(self, others):
        barrier = pltpu.get_barrier_semaphore()
        for p, t in others:
            pl.semaphore_signal(barrier, inc=1, device_id=(p, t), device_id_type=MESH)
        pl.semaphore_wait(barrier, len(others))

    def plane_others(self):
        return [(lax.rem(self.p + k, self.planes), self.t) for k in range(1, self.planes)]

    def time_others(self):
        return [(self.p, lax.rem(self.t + k, self.times)) for k in range(1, self.times)]

    def share_plane(self, blocks, send, recv):
        def start(k, carry):
            to = lax.rem(self.p + k, self.planes)
            self.copy(blocks.at[self.p], blocks.at[self.p], send.at[k], recv.at[self.p], p=to).start()
            return carry

        lax.fori_loop(1, self.planes, start, 0)

    def finish_plane(self, blocks, send, recv):
        def wait(k, carry):
            other = lax.rem(self.p + k, self.planes)
            self.copy(blocks.at[self.p], blocks.at[other], send.at[k], recv.at[other], p=other).wait()
            return carry

        lax.fori_loop(1, self.planes, wait, 0)

    def share_times(self, message, blocks, send, recv):
        def start(k, carry):
            to = lax.rem(self.t + k, self.times)
            self.copy(message, blocks.at[self.t], send.at[k], recv.at[self.t], t=to).start()
            return carry

        lax.fori_loop(1, self.times, start, 0)

    def finish_times(self, message, blocks, send, recv):
        def wait(k, carry):
            other = lax.rem(self.t + k, self.times)
            self.copy(message, blocks.at[other], send.at[k], recv.at[other], t=other).wait()
            return carry

        lax.fori_loop(1, self.times, wait, 0)


def total_of(blocks):
    total = blocks[0]
    for k in range(1, blocks.shape[0]):
        total = total + blocks[k]
    return total


def project_kernel(
    x_ref, f_ref, p_ref, g_ref,
    part, other, chip, acc, relay_in, direct_in, relay_out, joined_in,
    gram, gram_in, gram_all,
    pair_s, pair_r, ring_s, ring_r, ga_s, ga_r, gb_s, gb_r,
):
    me = Place()
    rows = acc.shape[1]
    half = rows // 2
    low, high = pl.ds(0, half), pl.ds(half, half)
    ring = me.ring
    me.greet(me.time_others() + me.plane_others())

    factors = f_ref[...]
    gram[...] = column_gram(factors, factors)
    slab = gram_in.shape[1]
    mine = gram.at[pl.ds(pl.multiple_of(me.p * slab, slab), slab)]
    me.share_times(mine, gram_in, ga_s, ga_r)
    gram_in[me.t] = mine[...]

    def block(owner):
        start = pl.multiple_of(owner * rows, rows)
        return jnp.dot(x_ref[pl.ds(start, rows), :], f_ref[...], preferred_element_type=F32)

    def to_pair(y):
        return me.copy(part.at[y], other.at[y], pair_s.at[y], pair_r.at[y], t=me.partner)

    def give(k, carry):
        y = me.ring_at(2 + 3 * k)
        part[y] = block(me.partner - me.t + me.time_of(y)).astype(BF16)
        to_pair(y).start()
        return carry

    lax.fori_loop(0, ring, give, 0)

    def chip_sum(y):
        own = block(me.time_of(y))
        to_pair(y).wait_recv()
        acc[y] = own + other[y].astype(F32)

    up, down, far = me.ring_at(1), me.ring_at(ring - 1), me.ring_at(2)
    t_up, t_down = me.time_of(up), me.time_of(down)

    chip_sum(far)
    chip[far] = acc[far].astype(BF16)
    relay_up = me.copy(chip.at[far, low], relay_in.at[0], ring_s.at[0], ring_r.at[0], t=t_up)
    relay_down = me.copy(chip.at[far, high], relay_in.at[1], ring_s.at[1], ring_r.at[1], t=t_down)
    relay_up.start()
    relay_down.start()
    chip_sum(up)
    chip[up, high] = acc[up, high].astype(BF16)
    direct_up = me.copy(chip.at[up, high], direct_in.at[0], ring_s.at[2], ring_r.at[2], t=t_up)
    direct_up.start()
    chip_sum(down)
    chip[down, low] = acc[down, low].astype(BF16)
    direct_down = me.copy(chip.at[down, low], direct_in.at[1], ring_s.at[3], ring_r.at[3], t=t_down)
    direct_down.start()

    me.finish_times(mine, gram_in, ga_s, ga_r)
    gram_all[me.p] = total_of(gram_in)
    me.share_plane(gram_all, gb_s, gb_r)

    chip_sum(me.y)

    relay_up.wait_recv()
    relay_out[0] = (acc[up, low] + relay_in[0].astype(F32)).astype(BF16)
    joined_up = me.copy(relay_out.at[0], joined_in.at[0], ring_s.at[4], ring_r.at[4], t=t_up)
    joined_up.start()
    relay_down.wait_recv()
    relay_out[1] = (acc[down, high] + relay_in[1].astype(F32)).astype(BF16)
    joined_down = me.copy(relay_out.at[1], joined_in.at[1], ring_s.at[5], ring_r.at[5], t=t_down)
    joined_down.start()

    me.finish_plane(gram_all, gb_s, gb_r)
    g_ref[...] = gram_all[...].reshape(g_ref.shape)

    direct_up.wait_recv()
    direct_down.wait_recv()
    joined_up.wait_recv()
    p_ref[low, :] = acc[me.y, low] + direct_in[1].astype(F32) + joined_in[0].astype(F32)
    joined_down.wait_recv()
    p_ref[high, :] = acc[me.y, high] + direct_in[0].astype(F32) + joined_in[1].astype(F32)

    for sent in (relay_up, relay_down, direct_up, direct_down, joined_up, joined_down):
        sent.wait_send()
    for y in range(ring):
        to_pair(y).wait_send()


def project(data, factors):
    planes, times = lax.axis_size("series"), lax.axis_size("tm")
    ring = times // 2
    n = factors.shape[1]
    rows = data.shape[0] // times
    half = rows // 2
    slab = n // planes
    return pl.pallas_call(
        project_kernel,
        out_shape=(jax.ShapeDtypeStruct((rows, n), F32), jax.ShapeDtypeStruct((n, n), F32)),
        in_specs=in_vmem(2),
        out_specs=tuple(in_vmem(2)),
        scratch_shapes=[
            pltpu.VMEM((ring, rows, n), BF16),
            pltpu.VMEM((ring, rows, n), BF16),
            pltpu.VMEM((ring, rows, n), BF16),
            pltpu.VMEM((ring, rows, n), F32),
            pltpu.VMEM((2, half, n), BF16),
            pltpu.VMEM((2, half, n), BF16),
            pltpu.VMEM((2, half, n), BF16),
            pltpu.VMEM((2, half, n), BF16),
            pltpu.VMEM((n, n), F32),
            pltpu.VMEM((times, slab, n), F32),
            pltpu.VMEM((planes, slab, n), F32),
            DMA((ring,)), DMA((ring,)), DMA((6,)), DMA((6,)),
            DMA((times,)), DMA((times,)), DMA((planes,)), DMA((planes,)),
        ],
        compiler_params=pltpu.CompilerParams(
            collective_id=0, has_side_effects=True, vmem_limit_bytes=32 * 1024 * 1024
        ),
        name="project",
    )(data, factors)


def cross_kernel(last, *refs):
    refs = list(refs)
    x_ref, l_ref, c_ref, g_ref = refs[:4]
    refs = refs[4:]
    if last:
        all_ref, square_ref = refs[:2]
        refs = refs[2:]
    lbuf, cacc, gacc, stacked, stacked_in, stacked_all = refs[:6]
    refs = refs[6:]
    pair_s, pair_r, ring_s, ring_r, ra_s, ra_r, rb_s, rb_r = refs[:8]
    me = Place()
    rows = l_ref.shape[0]
    half = rows // 2
    low, high = pl.ds(0, half), pl.ds(half, half)
    ring = me.ring
    up, down, far = me.ring_at(1), me.ring_at(ring - 1), me.ring_at(2)
    t_up, t_down, t_far = me.time_of(up), me.time_of(down), me.time_of(far)
    me.greet([(me.p, me.partner), (me.p, t_up), (me.p, t_down)] + me.plane_others())

    up_low = me.copy(l_ref.at[low], lbuf.at[me.t, low], ring_s.at[0], ring_r.at[0], t=t_up)
    down_high = me.copy(l_ref.at[high], lbuf.at[me.t, high], ring_s.at[1], ring_r.at[1], t=t_down)
    up_high = me.copy(l_ref.at[high], lbuf.at[me.t, high], ring_s.at[2], ring_r.at[2], t=t_up)
    down_low = me.copy(l_ref.at[low], lbuf.at[me.t, low], ring_s.at[3], ring_r.at[3], t=t_down)
    for sent in (up_low, down_high, up_high, down_low):
        sent.start()

    def to_pair(src, y):
        t = me.time_of(y)
        return me.copy(src, lbuf.at[t], pair_s.at[y], pair_r.at[y], t=me.partner)

    pair_own = to_pair(l_ref, me.y)
    pair_own.start()
    lbuf[me.t] = l_ref[...]
    cacc[...] = jnp.zeros_like(cacc)
    gacc[...] = jnp.zeros_like(gacc)

    def contribute(t):
        start = pl.multiple_of(t * rows, rows)
        loaded = lbuf[t]
        cacc[...] += column_gram(x_ref[pl.ds(start, rows), :], loaded)
        gacc[...] += column_gram(loaded, loaded)

    contribute(me.t)
    if last:
        def square(k, carry):
            start = pl.multiple_of(k * 64, 64)
            piece = x_ref[pl.ds(start, 64), :].astype(F32)
            piece = jnp.sum((piece * piece).reshape(8, 8, piece.shape[1]), axis=0)
            return carry + piece[:, : carry.shape[1]] + piece[:, carry.shape[1] :]

        square_ref[...] = lax.fori_loop(
            0, x_ref.shape[0] // 64, square, jnp.zeros(square_ref.shape, F32)
        )

    def across(y):
        other = me.partner - me.t + me.time_of(y)
        to_pair(lbuf.at[me.time_of(y)], y).wait_recv()
        contribute(other)

    across(me.y)
    up_low.wait_recv()
    far_up = me.copy(lbuf.at[t_down, low], lbuf.at[t_down, low], ring_s.at[4], ring_r.at[4], t=t_up)
    far_up.start()
    down_high.wait_recv()
    far_down = me.copy(lbuf.at[t_up, high], lbuf.at[t_up, high], ring_s.at[5], ring_r.at[5], t=t_down)
    far_down.start()
    up_high.wait_recv()
    pair_down = to_pair(lbuf.at[t_down], down)
    pair_down.start()
    down_low.wait_recv()
    pair_up = to_pair(lbuf.at[t_up], up)
    pair_up.start()
    contribute(t_down)
    contribute(t_up)
    across(down)
    across(up)
    far_up.wait_recv()
    far_down.wait_recv()
    pair_far = to_pair(lbuf.at[t_far], far)
    pair_far.start()
    contribute(t_far)
    across(far)

    c_slab, g_slab = c_ref.shape[0] // me.planes, g_ref.shape[0] // me.planes
    n = g_ref.shape[1]
    stacked[:, :c_slab, :] = cacc[...].reshape(me.planes, c_slab, n)
    stacked[:, c_slab:, :] = gacc[...].reshape(me.planes, g_slab, n)

    def start(k, carry):
        to = lax.rem(me.p + k, me.planes)
        me.copy(stacked.at[to], stacked_in.at[me.p], ra_s.at[k], ra_r.at[me.p], p=to).start()
        return carry

    def wait(k, carry):
        other = lax.rem(me.p + k, me.planes)
        me.copy(stacked.at[other], stacked_in.at[other], ra_s.at[k], ra_r.at[other], p=other).wait()
        return carry

    lax.fori_loop(1, me.planes, start, 0)
    if last:
        saved = pltpu.make_async_copy(lbuf, all_ref, refs[8])
        saved.start()
    stacked_in[me.p] = stacked[me.p]
    lax.fori_loop(1, me.planes, wait, 0)
    stacked_all[me.p] = total_of(stacked_in)
    me.share_plane(stacked_all, rb_s, rb_r)
    for sent in (up_low, down_high, up_high, down_low, far_up, far_down):
        sent.wait_send()
    for sent in (pair_own, pair_down, pair_up, pair_far):
        sent.wait_send()
    me.finish_plane(stacked_all, rb_s, rb_r)
    c_ref[...] = stacked_all[:, :c_slab, :].reshape(c_ref.shape)
    g_ref[...] = stacked_all[:, c_slab:, :].reshape(g_ref.shape)
    if last:
        saved.wait()


def cross_and_gram(data, share, last):
    planes, times = lax.axis_size("series"), lax.axis_size("tm")
    ring = times // 2
    rows, n = share.shape
    span = data.shape[1]
    tall = span // planes + n // planes
    out_shape = [jax.ShapeDtypeStruct((span, n), F32), jax.ShapeDtypeStruct((n, n), F32)]
    out_specs = in_vmem(2)
    extra = []
    if last:
        out_shape += [
            jax.ShapeDtypeStruct((times, rows, n), BF16),
            jax.ShapeDtypeStruct((8, n), F32),
        ]
        out_specs += [pl.BlockSpec(memory_space=pl.ANY), pl.BlockSpec(memory_space=pltpu.VMEM)]
        extra = [DMA]
    return pl.pallas_call(
        functools.partial(cross_kernel, last),
        out_shape=tuple(out_shape),
        in_specs=in_vmem(2),
        out_specs=tuple(out_specs),
        scratch_shapes=[
            pltpu.VMEM((times, rows, n), BF16),
            pltpu.VMEM((span, n), F32),
            pltpu.VMEM((n, n), F32),
            pltpu.VMEM((planes, tall, n), F32),
            pltpu.VMEM((planes, tall, n), F32),
            pltpu.VMEM((planes, tall, n), F32),
            DMA((ring,)), DMA((ring,)), DMA((6,)), DMA((6,)),
            DMA((planes,)), DMA((planes,)), DMA((planes,)), DMA((planes,)),
        ]
        + extra,
        compiler_params=pltpu.CompilerParams(
            collective_id=2 if last else 1,
            has_side_effects=True,
            vmem_limit_bytes=32 * 1024 * 1024,
        ),
        name="cross_last" if last else "cross",
    )(data, share)


def tail_kernel(
    f_ref, c_ref, gl_ref, square_ref, lag_ref, base_ref, earlier_ref, sums_ref,
    before, lag, base, message, message_in, message_all,
    row_s, row_r, ta_s, ta_r, tb_s, tb_r,
):
    me = Place()
    span, n = f_ref.shape
    edge = before.shape[0]
    me.greet(me.time_others() + me.plane_others())
    following = lax.rem(me.t + 1, me.times)
    row = me.copy(f_ref.at[pl.ds(span - edge, edge)], before, row_s, row_r, t=following)
    row.start()
    factors = f_ref[...]
    wide_factors = factors.astype(F32)
    expanded = gl_ref[...] * column_gram(factors, factors)
    fitted = -2.0 * wide_factors * c_ref[...]
    share = jnp.sum(expanded.reshape(n // 8, 8, n), axis=0)
    share = share + jnp.sum(fitted.reshape(span // 8, 8, n), axis=0)
    rolled = pltpu.roll(wide_factors, 1, 0)
    first = lax.broadcasted_iota(jnp.int32, (span, n), 0) == 0
    row.wait()
    head = before[...].astype(F32)[edge - 1 :, :]
    head = head * jnp.where(me.t == 0, 0.0, 1.0)
    earlier = jnp.where(first, head, rolled).astype(BF16)
    earlier_ref[...] = earlier
    lag[...] = column_gram(factors, earlier)
    base[...] = column_gram(earlier, earlier)
    slab = n // me.planes
    here = pl.ds(pl.multiple_of(me.p * slab, slab), slab)
    message[:slab, :] = lag[here, :]
    message[slab : 2 * slab, :] = base[here, :]
    message[2 * slab : 2 * slab + 8, :] = share
    message[2 * slab + 8 :, :] = square_ref[...]
    me.share_times(message, message_in, ta_s, ta_r)
    message_in[me.t] = message[...]
    me.finish_times(message, message_in, ta_s, ta_r)
    message_all[me.p] = total_of(message_in)
    me.share_plane(message_all, tb_s, tb_r)
    me.finish_plane(message_all, tb_s, tb_r)
    lag_ref[...] = message_all[:, :slab, :].reshape(n, n)
    base_ref[...] = message_all[:, slab : 2 * slab, :].reshape(n, n)
    sums_ref[:8, :] = message_all[0, 2 * slab : 2 * slab + 8, :]
    sums_ref[8:, :] = total_of(message_all[:, 2 * slab + 8 :, :])


def tail(factors, cross, gram_loadings, squares):
    planes, times = lax.axis_size("series"), lax.axis_size("tm")
    span, n = factors.shape
    tall = 2 * (n // planes) + 16
    square = jax.ShapeDtypeStruct((n, n), F32)
    return pl.pallas_call(
        tail_kernel,
        out_shape=(
            square,
            square,
            jax.ShapeDtypeStruct((span, n), BF16),
            jax.ShapeDtypeStruct((16, n), F32),
        ),
        in_specs=in_vmem(4),
        out_specs=tuple(in_vmem(4)),
        scratch_shapes=[
            pltpu.VMEM((16, n), BF16),
            pltpu.VMEM((n, n), F32),
            pltpu.VMEM((n, n), F32),
            pltpu.VMEM((tall, n), F32),
            pltpu.VMEM((times, tall, n), F32),
            pltpu.VMEM((planes, tall, n), F32),
            DMA, DMA, DMA((times,)), DMA((times,)), DMA((planes,)), DMA((planes,)),
        ],
        compiler_params=pltpu.CompilerParams(
            collective_id=3, has_side_effects=True, vmem_limit_bytes=32 * 1024 * 1024
        ),
        name="tail",
    )(factors, cross, gram_loadings, squares)


def fit_kernel(
    lag_ref, base_ref, f_ref, earlier_ref, sums_ref, move_ref, news_ref, share_ref, a_ref, x_ref, e_ref
):
    inverse = inverse_of(base_ref, a_ref, x_ref, e_ref)
    move = wide(lag_ref[...], inverse)
    move_ref[...] = move
    predicted = lax.dot_general(
        earlier_ref[...].astype(F32),
        move,
        (((1,), (1,)), ((), ())),
        precision=lax.Precision.HIGHEST,
        preferred_element_type=F32,
    )
    news_ref[...] = f_ref[...].astype(F32) - predicted
    total = jnp.sum(sums_ref[8:, :])
    share_ref[0, 0] = (total + jnp.sum(sums_ref[:8, :])) / total


def fit(lagged, base, factors, earlier, sums):
    span, n = factors.shape
    square = pltpu.VMEM((n, n), F32)
    return pl.pallas_call(
        fit_kernel,
        out_shape=(
            jax.ShapeDtypeStruct((n, n), F32),
            jax.ShapeDtypeStruct((span, n), F32),
            jax.ShapeDtypeStruct((1, 1), F32),
        ),
        in_specs=in_vmem(5),
        out_specs=(*in_vmem(2), pl.BlockSpec(memory_space=pltpu.SMEM)),
        scratch_shapes=[square] * 3,
        compiler_params=pltpu.CompilerParams(vmem_limit_bytes=16 * 1024 * 1024),
        name="fit",
    )(lagged, base, factors, earlier, sums)


def body(data, factors_init):
    factors = factors_init
    for sweep in range(ITERS):
        last = sweep == ITERS - 1
        projection, gram_factors = project(data, factors)
        share = solve(gram_factors, projection)
        cross, gram_loadings, *extra = cross_and_gram(data, share, last)
        factors = solve(gram_loadings, cross)
    gathered, squares = extra
    loadings = gathered.reshape(data.shape[0], factors.shape[1])
    lagged, base, earlier, sums = tail(factors, cross, gram_loadings, squares)
    transition, innovations, residual_share = fit(lagged, base, factors, earlier, sums)
    return (loadings, factors, innovations, transition, residual_share.reshape(()))


def solution(mesh):
    return jax.shard_map(
        body,
        mesh=mesh,
        in_specs=(P("series", "tm"), P("tm", None)),
        out_specs=(P("series", None), P("tm", None), P("tm", None), P(), P()),
        check_vma=False,
    )
```

time: 773 us -> 269 us (0.35); the launches traced: 762 us -> 268 us
  waiting for transfers between devices: 467 us -> 0 us
  Pallas kernels: 36.4 us -> 261 us
  blocking collectives: 121 us -> 0 us
  starting transfers between devices: 40.2 us -> 0 us
  matrix products: 35.3 us -> 0 us
  other arithmetic: 20.3 us -> 0 us
  between operations: 19 us -> 0.74 us
  local copies, waits for them, and re-layouts: 22.8 us -> 5.4 us
    psum x4 -> x0, waiting for transfers between devices: 278 us -> none  [the longest x3 252 us: body(): lax.psum((loading_part, cross_part, data_block), 'series')]
    pallas_call x7 -> x14, Pallas kernels: 36.4 us -> 261 us  [the longest x3 111 us: cross_and_gram(): pl.pallas_call(functools.partial(cross_kernel, last), out_shape=tuple(out...]
    all_to_all x6 -> x0, waiting for transfers between devices: 189 us -> none  [the longest x3 128 us: sum_at_owner(): lax.all_to_all(tiles, axis, split_axis=0, concat_axis=0, tiled=True)]
    all_to_all x3 -> x0, blocking collectives: 89.7 us -> none  [sent_to_all(): return lax.all_to_all(copies, axis, split_axis=0, concat_axis=0, tiled=True)]
    dot_general x23 -> x0, matrix products: 35.3 us -> none  [the longest x12 12.9 us: column_gram(): lax.dot_general(left, right, (((0,), (0,)), ((), ())), preferred_element_...]
    all_to_all x6 -> x0, starting transfers between devices: 35 us -> none  [the longest x3 18.8 us: sent_to_all(): return lax.all_to_all(copies, axis, split_axis=0, concat_axis=0, tiled=True)]
    psum x1 -> x0, blocking collectives: 31.5 us -> none  [body(): lax.psum((loading_part, cross_part, data_block), 'series')]
    reduce_sum x7 -> x0, other arithmetic: 17.4 us -> none  [the longest x3 7.91 us: sum_at_owner(): return arrived.sum(axis=0)]
  transfers between devices with their start and end apart: 11 -> 0, of which waited for: 10 -> 0; matrix products, arithmetic and copies ran while one was open for 3% -> 0% of each run, Pallas kernels for 2% -> 0%
where the time goes in v1:
time: 269 us; the launch traced here: 268 us
  Pallas kernels  261 us (97%)
  local copies, waits for them, and re-layouts  5.4 us (2%)
    pallas_call x3, Pallas kernels, cross_and_gram(): pl.pallas_call(functools.partial(cross_kernel, last), out_shape=tuple(out...  111 us
    pallas_call x3, Pallas kernels, project(): pl.pallas_call(project_kernel, out_shape=(jax.ShapeDtypeStruct((rows, n),...  66.9 us
    pallas_call x6, Pallas kernels, solve(): pl.pallas_call(solve_kernel, out_shape=jax.ShapeDtypeStruct(rows.shape, B...  49.7 us
    pallas_call x1, Pallas kernels, tail(): pl.pallas_call(tail_kernel, out_shape=(square, square, jax.ShapeDtypeStru...  27.2 us
    pallas_call x1, Pallas kernels, fit(): pl.pallas_call(fit_kernel, out_shape=(jax.ShapeDtypeStruct((n, n), F32),...  6.47 us
    unnamed x7, local copies, waits for them, and re-layouts  5.4 us

profile of v1, /device:TPU:1, one launch (start us, length us, event | category | flops | bytes accessed | tf_op | source)
XLA Modules:
  0.0 267.5 jit_solution(4480794472031553374)
XLA Ops:
  0.6 0.0 copy-start
  0.6 2.2 copy-done
  2.8 0.0 copy-start.2
  2.8 0.9 copy-done.2
  3.8 23.1 %project.3 = (f32[512,256]{1,0:T(8,128)S(1)}, f32[256,256]{1,0:T(8,128)S(1)}) custom-call(bf16[4096,512]{1,0:T(8,128)(2,1)S(1)} %copy-done, bf16[512,256]{1,0:T(8,128)(2,1)S(1)} %copy-done.2), custom_call_target="tpu_custom_call" | custom-call | tf_op jit(solution)/shard_map/project/pallas_call | solution.py:298
  26.9 5.0 %solve.6.refs_1_ = bf16[512,256]{1,0:T(8,128)(2,1)S(1)} custom-call(f32[256,256]{1,0:T(8,128)S(1)} %get-tuple-element.26.g_ref, f32[512,256]{1,0:T(8,128)S(1)} %get-tuple-element.27.m_ref), custom_call_target="tpu_custom_call" | custom-call | tf_op jit(solution)/shard_map/solve/pallas_call | solution.py:112
  31.8 36.8 %cross.2 = (f32[512,256]{1,0:T(8,128)S(1)}, f32[256,256]{1,0:T(8,128)S(1)}) custom-call(bf16[4096,512]{1,0:T(8,128)(2,1)S(1)} %copy-done, bf16[512,256]{1,0:T(8,128)(2,1)S(1)} %solve.6.refs_1_), custom_call_target="tpu_custom_call" | custom-call | tf_op jit(solution)/shard_map/cross/pallas_call | solution.py:458
  68.7 6.9 %solve.7.f_ref = bf16[512,256]{1,0:T(8,128)(2,1)S(1)} custom-call(f32[256,256]{1,0:T(8,128)S(1)} %get-tuple-element.28.g_ref, f32[512,256]{1,0:T(8,128)S(1)} %get-tuple-element.29.m_ref), custom_call_target="tpu_custom_call" | custom-call | tf_op jit(solution)/shard_map/solve/pallas_call | solution.py:112
  75.6 21.9 %project.4 = (f32[512,256]{1,0:T(8,128)S(1)}, f32[256,256]{1,0:T(8,128)S(1)}) custom-call(bf16[4096,512]{1,0:T(8,128)(2,1)S(1)} %copy-done, bf16[512,256]{1,0:T(8,128)(2,1)S(1)} %solve.7.f_ref), custom_call_target="tpu_custom_call" | custom-call | tf_op jit(solution)/shard_map/project/pallas_call | solution.py:298
  97.5 5.0 %solve.8.refs_1_ = bf16[512,256]{1,0:T(8,128)(2,1)S(1)} custom-call(f32[256,256]{1,0:T(8,128)S(1)} %get-tuple-element.30.g_ref, f32[512,256]{1,0:T(8,128)S(1)} %get-tuple-element.31.m_ref), custom_call_target="tpu_custom_call" | custom-call | tf_op jit(solution)/shard_map/solve/pallas_call | solution.py:112
  102.4 37.1 %cross.3 = (f32[512,256]{1,0:T(8,128)S(1)}, f32[256,256]{1,0:T(8,128)S(1)}) custom-call(bf16[4096,512]{1,0:T(8,128)(2,1)S(1)} %copy-done, bf16[512,256]{1,0:T(8,128)(2,1)S(1)} %solve.8.refs_1_), custom_call_target="tpu_custom_call" | custom-call | tf_op jit(solution)/shard_map/cross/pallas_call | solution.py:458
  139.6 6.9 %solve.9.f_ref = bf16[512,256]{1,0:T(8,128)(2,1)S(1)} custom-call(f32[256,256]{1,0:T(8,128)S(1)} %get-tuple-element.32.g_ref, f32[512,256]{1,0:T(8,128)S(1)} %get-tuple-element.33.m_ref), custom_call_target="tpu_custom_call" | custom-call | tf_op jit(solution)/shard_map/solve/pallas_call | solution.py:112
  146.5 21.9 %project.5 = (f32[512,256]{1,0:T(8,128)S(1)}, f32[256,256]{1,0:T(8,128)S(1)}) custom-call(bf16[4096,512]{1,0:T(8,128)(2,1)S(1)} %copy-done, bf16[512,256]{1,0:T(8,128)(2,1)S(1)} %solve.9.f_ref), custom_call_target="tpu_custom_call" | custom-call | tf_op jit(solution)/shard_map/project/pallas_call | solution.py:298
  168.4 5.0 %solve.10.refs_1_ = bf16[512,256]{1,0:T(8,128)(2,1)S(1)} custom-call(f32[256,256]{1,0:T(8,128)S(1)} %get-tuple-element.34.g_ref, f32[512,256]{1,0:T(8,128)S(1)} %get-tuple-element.35.m_ref), custom_call_target="tpu_custom_call" | custom-call | tf_op jit(solution)/shard_map/solve/pallas_call | solution.py:112
  173.3 37.2 %cross_last.1 = (f32[512,256]{1,0:T(8,128)S(1)}, f32[256,256]{1,0:T(8,128)S(1)}, bf16[8,512,256]{2,1,0:T(8,128)(2,1)S(1)}, f32[8,256]{1,0:T(8,128)S(1)}) custom-call(bf16[4096,512]{1,0:T(8,128)(2,1)S(1)} %copy-done, bf16[512,256]{1,0:T(8,128)(2,1)S(1)} %solve.10.refs_1_), custom_call_target="tpu_custom_call" | custom-call | tf_op jit(solution)/shard_map/cross_last/pallas_call | solution.py:458
  210.5 21.1 %solve.11.f_ref = bf16[512,256]{1,0:T(8,128)(2,1)} custom-call(f32[256,256]{1,0:T(8,128)S(1)} %get-tuple-element.37.g_ref.gl_ref, f32[512,256]{1,0:T(8,128)S(1)} %get-tuple-element.38.m_ref.c_ref), custom_call_target="tpu_custom_call" | custom-call | tf_op jit(solution)/shard_map/solve/pallas_call | solution.py:112
  231.6 0.0 copy-start.1
  231.6 0.9 copy-done.1
  232.5 27.2 %tail.1 = (f32[256,256]{1,0:T(8,128)S(1)}, f32[256,256]{1,0:T(8,128)S(1)}, bf16[512,256]{1,0:T(8,128)(2,1)S(1)}, f32[16,256]{1,0:T(8,128)S(1)}) custom-call(bf16[512,256]{1,0:T(8,128)(2,1)S(1)} %copy-done.1, f32[512,256]{1,0:T(8,128)S(1)} %get-tuple-element.38.m_ref.c_ref, f32[256,256]{1,0:T(8,128)S(1)} %get-tuple-element.37.g_ref.gl_ref, ...), custom_call_target="tpu_custom_call" | custom-call | tf_op jit(solution)/shard_map/tail/pallas_call | solution.py:533
  259.7 6.5 %fit.1 = (f32[256,256]{1,0:T(8,128)}, f32[512,256]{1,0:T(8,128)}, f32[1,1]{1,0:T(1,128)}) custom-call(f32[256,256]{1,0:T(8,128)S(1)} %get-tuple-element.40.lag_ref, f32[256,256]{1,0:T(8,128)S(1)} %get-tuple-element.41.base_ref, bf16[512,256]{1,0:T(8,128)(2,1)S(1)} %copy-done.1, bf16[512,256]{1,0:T(8,128)(2,1)S(1)} %get-tuple-element.42.earlier_ref, ...), custom_call_target="tpu_custom_call" | custom-call | tf_op jit(solution)/shard_map/fit/pallas_call | solution.py:580
  266.2 1.3 copy.8
Async XLA Ops:
  0.6 2.2 copy-start
  2.8 0.9 copy-start.2
  231.6 0.9 copy-start.1

commit v2 on v1

v2 whole, which is shorter than its diff:
```python
import functools

import jax
import jax.numpy as jnp
from jax import lax
from jax.experimental import pallas as pl
from jax.experimental.pallas import tpu as pltpu
from jax.sharding import PartitionSpec as P

ITERS = 3
RIDGE = 0.01
MESH = pl.DeviceIdType.MESH
F32 = jnp.float32
BF16 = jnp.bfloat16
DMA = pltpu.SemaphoreType.DMA


def narrow(left, right):
    return jnp.dot(left.astype(BF16), right.astype(BF16), preferred_element_type=F32)


def wide(left, right):
    return jnp.dot(left, right, precision=lax.Precision.HIGHEST, preferred_element_type=F32)


def column_gram(left, right):
    return lax.dot_general(left, right, (((0,), (0,)), ((), ())), preferred_element_type=F32)


def inverse_of(gram, a_ref, x_ref, e_ref):
    n = gram.shape[0]
    rows = lax.broadcasted_iota(jnp.int32, (n, n), 0)
    cols = lax.broadcasted_iota(jnp.int32, (n, n), 1)
    diagonal = rows == cols
    masked = jnp.where(diagonal, gram, 0.0)
    down = lax.rsqrt(jnp.sum(masked, axis=1, keepdims=True))
    across = lax.rsqrt(jnp.sum(masked, axis=0, keepdims=True))
    scaled = gram * down * across
    a_ref[...] = scaled
    bound = jnp.max(jnp.sum(jnp.abs(scaled), axis=0, keepdims=True))
    alpha = 1.9 / bound
    start = jnp.where(diagonal, alpha, 0.0)
    x_ref[...] = start
    e_ref[...] = jnp.where(diagonal, 1.0, 0.0) - alpha * scaled

    def squaring(carry):
        step, _ = carry
        for _ in range(2):
            error = e_ref[...]
            guess = x_ref[...]
            e_ref[...] = narrow(error, error)
            x_ref[...] = guess + narrow(guess, error)
        final = e_ref[...]
        return step + 1, jnp.sum(final * final)

    lax.while_loop(
        lambda c: jnp.logical_and(c[0] < 10, jnp.logical_and(c[1] > 1e-2, c[1] < 1e3)),
        squaring,
        (0, jnp.float32(1.0)),
    )

    def residual():
        error = jnp.where(diagonal, 1.0, 0.0) - wide(a_ref[...], x_ref[...])
        e_ref[...] = error
        return jnp.max(jnp.abs(error))

    def refine(carry):
        step, _ = carry
        worst = residual()
        guess = x_ref[...]
        x_ref[...] = guess + narrow(guess, e_ref[...])
        return step + 1, worst

    _, worst = lax.while_loop(
        lambda c: jnp.logical_and(c[0] < 8, jnp.logical_and(c[1] >= 5e-4, c[1] < 2.0)),
        refine,
        (0, jnp.float32(1.0)),
    )

    @pl.when(worst >= 5e-4)
    def _():
        x_ref[...] = jnp.where(diagonal, alpha, 0.0)

        def newton(carry):
            step, _ = carry
            error = residual()
            guess = x_ref[...]
            x_ref[...] = guess + wide(guess, e_ref[...])
            return step + 1, error

        lax.while_loop(
            lambda c: jnp.logical_and(c[0] < 48, c[1] >= 5e-4),
            newton,
            (0, jnp.float32(1.0)),
        )

    return x_ref[...] * down * across


class Place:
    def __init__(self):
        self.p = lax.axis_index("series")
        self.t = lax.axis_index("tm")
        self.planes = lax.axis_size("series")
        self.times = lax.axis_size("tm")
        self.ring = self.times // 2
        self.y = lax.div(self.t, 2)
        self.c = lax.rem(self.t, 2)
        self.partner = self.t + 1 - 2 * self.c

    def ring_at(self, distance):
        return lax.rem(self.y + distance, self.ring)

    def time_of(self, y):
        return 2 * y + self.c

    def copy(self, src, dst, send, recv, p=None, t=None):
        return pltpu.make_async_remote_copy(
            src_ref=src,
            dst_ref=dst,
            send_sem=send,
            recv_sem=recv,
            device_id=(self.p if p is None else p, self.t if t is None else t),
            device_id_type=MESH,
        )

    def greet(self, others):
        barrier = pltpu.get_barrier_semaphore()
        for p, t in others:
            pl.semaphore_signal(barrier, inc=1, device_id=(p, t), device_id_type=MESH)
        pl.semaphore_wait(barrier, len(others))

    def plane_others(self):
        return [(lax.rem(self.p + k, self.planes), self.t) for k in range(1, self.planes)]

    def time_others(self):
        return [(self.p, lax.rem(self.t + k, self.times)) for k in range(1, self.times)]

    def share_plane(self, message, blocks, send, recv):
        def start(k, carry):
            to = lax.rem(self.p + k, self.planes)
            self.copy(message, blocks.at[self.p], send.at[k], recv.at[self.p], p=to).start()
            return carry

        lax.fori_loop(1, self.planes, start, 0)

    def finish_plane(self, message, blocks, send, recv):
        def wait(k, carry):
            other = lax.rem(self.p + k, self.planes)
            self.copy(message, blocks.at[other], send.at[k], recv.at[other], p=other).wait()
            return carry

        lax.fori_loop(1, self.planes, wait, 0)

    def spread_plane(self, pieces, blocks, send, recv):
        def start(k, carry):
            to = lax.rem(self.p + k, self.planes)
            self.copy(pieces.at[to], blocks.at[self.p], send.at[k], recv.at[self.p], p=to).start()
            return carry

        lax.fori_loop(1, self.planes, start, 0)

    def finish_spread(self, pieces, blocks, send, recv):
        def wait(k, carry):
            other = lax.rem(self.p + k, self.planes)
            self.copy(pieces.at[other], blocks.at[other], send.at[k], recv.at[other], p=other).wait()
            return carry

        lax.fori_loop(1, self.planes, wait, 0)

    def share_times(self, message, blocks, send, recv):
        def start(k, carry):
            to = lax.rem(self.t + k, self.times)
            self.copy(message, blocks.at[self.t], send.at[k], recv.at[self.t], t=to).start()
            return carry

        lax.fori_loop(1, self.times, start, 0)

    def finish_times(self, message, blocks, send, recv):
        def wait(k, carry):
            other = lax.rem(self.t + k, self.times)
            self.copy(message, blocks.at[other], send.at[k], recv.at[other], t=other).wait()
            return carry

        lax.fori_loop(1, self.times, wait, 0)


def total_of(blocks):
    total = blocks[0]
    for k in range(1, blocks.shape[0]):
        total = total + blocks[k]
    return total


def in_vmem(count):
    return [pl.BlockSpec(memory_space=pltpu.VMEM)] * count


def sweep_kernel(first, last, *refs):
    refs = list(refs)

    def take(count):
        taken, refs[:] = refs[:count], refs[count:]
        return taken

    x_ref, f_ref, w_ref, m_ref, g_ref = take(5)
    if last:
        all_ref, square_ref = take(2)
    if not first:
        fbuf, f_s, f_r = take(3)
    part, other, chip, acc, relay_in, direct_in, relay_out, joined_in = take(8)
    gram, gram_in, gram_all, moment, moment_in, moment_own, moment_times, moment_all = take(8)
    pbuf, wacc, winc = take(3)
    pair_s, pair_r, ring_s, ring_r, ga_s, ga_r, gb_s, gb_r = take(8)
    gpair_s, gpair_r, gring_s, gring_r, ma_s, ma_r, mb_s, mb_r, mc_s, mc_r, w_s, w_r = take(12)
    me = Place()
    rows = acc.shape[1]
    half = rows // 2
    low, high = pl.ds(0, half), pl.ds(half, half)
    ring = me.ring
    up, down, far = me.ring_at(1), me.ring_at(ring - 1), me.ring_at(2)
    t_up, t_down, t_far = me.time_of(up), me.time_of(down), me.time_of(far)
    slab = gram_in.shape[1]
    me.greet(me.time_others() + me.plane_others())

    if first:
        def factors():
            return f_ref[...]
    else:
        me.share_plane(f_ref, fbuf, f_s, f_r)
        fbuf[me.p] = f_ref[...]
        me.finish_plane(f_ref, fbuf, f_s, f_r)

        def factors():
            return fbuf[...].reshape(x_ref.shape[1], f_ref.shape[1])

    gram[...] = column_gram(factors(), factors())
    mine = gram.at[pl.ds(pl.multiple_of(me.p * slab, slab), slab)]
    me.share_times(mine, gram_in, ga_s, ga_r)
    gram_in[me.t] = mine[...]

    def block(owner):
        start = pl.multiple_of(owner * rows, rows)
        return jnp.dot(x_ref[pl.ds(start, rows), :], factors(), preferred_element_type=F32)

    def to_pair(y):
        return me.copy(part.at[y], other.at[y], pair_s.at[y], pair_r.at[y], t=me.partner)

    def give(k, carry):
        y = me.ring_at(2 + 3 * k)
        part[y] = block(me.partner - me.t + me.time_of(y)).astype(BF16)
        to_pair(y).start()
        return carry

    lax.fori_loop(0, ring, give, 0)

    def chip_sum(y):
        own = block(me.time_of(y))
        to_pair(y).wait_recv()
        acc[y] = own + other[y].astype(F32)

    chip_sum(far)
    chip[far] = acc[far].astype(BF16)
    relay_up = me.copy(chip.at[far, low], relay_in.at[0], ring_s.at[0], ring_r.at[0], t=t_up)
    relay_down = me.copy(chip.at[far, high], relay_in.at[1], ring_s.at[1], ring_r.at[1], t=t_down)
    relay_up.start()
    relay_down.start()
    chip_sum(up)
    chip[up, high] = acc[up, high].astype(BF16)
    direct_up = me.copy(chip.at[up, high], direct_in.at[0], ring_s.at[2], ring_r.at[2], t=t_up)
    direct_up.start()
    chip_sum(down)
    chip[down, low] = acc[down, low].astype(BF16)
    direct_down = me.copy(chip.at[down, low], direct_in.at[1], ring_s.at[3], ring_r.at[3], t=t_down)
    direct_down.start()
    chip_sum(me.y)

    relay_up.wait_recv()
    relay_out[0] = (acc[up, low] + relay_in[0].astype(F32)).astype(BF16)
    joined_up = me.copy(relay_out.at[0], joined_in.at[0], ring_s.at[4], ring_r.at[4], t=t_up)
    joined_up.start()
    relay_down.wait_recv()
    relay_out[1] = (acc[down, high] + relay_in[1].astype(F32)).astype(BF16)
    joined_down = me.copy(relay_out.at[1], joined_in.at[1], ring_s.at[5], ring_r.at[5], t=t_down)
    joined_down.start()

    me.finish_times(mine, gram_in, ga_s, ga_r)
    gram_all[me.p] = total_of(gram_in)
    me.share_plane(gram_all.at[me.p], gram_all, gb_s, gb_r)

    direct_up.wait_recv()
    direct_down.wait_recv()
    joined_up.wait_recv()
    pbuf[me.t, low] = (
        acc[me.y, low] + direct_in[1].astype(F32) + joined_in[0].astype(F32)
    ).astype(BF16)
    mine_low, mine_high = pbuf.at[me.t, low], pbuf.at[me.t, high]
    up_low = me.copy(mine_low, mine_low, gring_s.at[0], gring_r.at[0], t=t_up)
    up_low.start()
    joined_down.wait_recv()
    pbuf[me.t, high] = (
        acc[me.y, high] + direct_in[0].astype(F32) + joined_in[1].astype(F32)
    ).astype(BF16)
    down_high = me.copy(mine_high, mine_high, gring_s.at[1], gring_r.at[1], t=t_down)
    down_high.start()
    up_high = me.copy(mine_high, mine_high, gring_s.at[2], gring_r.at[2], t=t_up)
    up_high.start()
    down_low = me.copy(mine_low, mine_low, gring_s.at[3], gring_r.at[3], t=t_down)
    down_low.start()

    def pass_over(y):
        piece = pbuf.at[me.time_of(y)]
        return me.copy(piece, piece, gpair_s.at[y], gpair_r.at[y], t=me.partner)

    pass_over(me.y).start()

    own_rows = pbuf[me.t]
    moment[...] = column_gram(own_rows, own_rows).reshape(moment.shape)
    me.spread_plane(moment, moment_in, ma_s, ma_r)
    moment_in[me.p] = moment[me.p]

    wacc[...] = jnp.zeros_like(wacc)

    def contribute(t):
        start = pl.multiple_of(t * rows, rows)
        wacc[...] += column_gram(x_ref[pl.ds(start, rows), :], pbuf[t]).reshape(wacc.shape)

    def across(y):
        pass_over(y).wait_recv()
        contribute(me.partner - me.t + me.time_of(y))

    contribute(me.t)
    across(me.y)
    if last:
        def square(k, carry):
            start = pl.multiple_of(k * 64, 64)
            piece = x_ref[pl.ds(start, 64), :].astype(F32)
            piece = jnp.sum((piece * piece).reshape(8, 8, piece.shape[1]), axis=0)
            return carry + piece[:, : carry.shape[1]] + piece[:, carry.shape[1] :]

        square_ref[...] = lax.fori_loop(
            0, x_ref.shape[0] // 64, square, jnp.zeros(square_ref.shape, F32)
        )
    up_low.wait_recv()
    far_low = pbuf.at[t_down, low]
    far_up = me.copy(far_low, far_low, gring_s.at[4], gring_r.at[4], t=t_up)
    far_up.start()
    down_high.wait_recv()
    far_high = pbuf.at[t_up, high]
    far_down = me.copy(far_high, far_high, gring_s.at[5], gring_r.at[5], t=t_down)
    far_down.start()

    me.finish_spread(moment, moment_in, ma_s, ma_r)
    moment_own[...] = total_of(moment_in)
    me.share_times(moment_own, moment_times, mb_s, mb_r)
    moment_times[me.t] = moment_own[...]

    up_high.wait_recv()
    pass_over(down).start()
    down_low.wait_recv()
    pass_over(up).start()
    contribute(t_down)
    contribute(t_up)
    across(down)
    across(up)
    me.finish_times(moment_own, moment_times, mb_s, mb_r)
    moment_all[me.p] = total_of(moment_times)
    me.share_plane(moment_all.at[me.p], moment_all, mc_s, mc_r)
    far_up.wait_recv()
    far_down.wait_recv()
    pass_over(far).start()
    contribute(t_far)
    across(far)

    me.spread_plane(wacc, winc, w_s, w_r)
    winc[me.p] = wacc[me.p]
    if last:
        all_ref[...] = pbuf[...]
    me.finish_plane(gram_all.at[me.p], gram_all, gb_s, gb_r)
    g_ref[...] = gram_all[...].reshape(g_ref.shape)
    me.finish_plane(moment_all.at[me.p], moment_all, mc_s, mc_r)
    m_ref[...] = moment_all[...].reshape(m_ref.shape)
    me.finish_spread(wacc, winc, w_s, w_r)
    w_ref[...] = total_of(winc)

    for sent in (relay_up, relay_down, direct_up, direct_down, joined_up, joined_down):
        sent.wait_send()
    for sent in (up_low, down_high, up_high, down_low, far_up, far_down):
        sent.wait_send()
    for y in range(ring):
        to_pair(y).wait_send()
        pass_over(y).wait_send()


def sweep(data, factors, first, last):
    planes, times = lax.axis_size("series"), lax.axis_size("tm")
    ring = times // 2
    n = factors.shape[1]
    span = data.shape[1]
    rows = data.shape[0] // times
    half = rows // 2
    slab, tall = n // planes, span // planes
    out_shape = [
        jax.ShapeDtypeStruct((tall, n), F32),
        jax.ShapeDtypeStruct((n, n), F32),
        jax.ShapeDtypeStruct((n, n), F32),
    ]
    if last:
        out_shape += [
            jax.ShapeDtypeStruct((times, rows, n), BF16),
            jax.ShapeDtypeStruct((8, n), F32),
        ]
    scratch = []
    if not first:
        scratch += [pltpu.VMEM((planes, tall, n), BF16), DMA((planes,)), DMA((planes,))]
    scratch += [pltpu.VMEM((ring, rows, n), BF16)] * 3 + [pltpu.VMEM((ring, rows, n), F32)]
    scratch += [pltpu.VMEM((2, half, n), BF16)] * 4
    scratch += [
        pltpu.VMEM((n, n), F32),
        pltpu.VMEM((times, slab, n), F32),
        pltpu.VMEM((planes, slab, n), F32),
        pltpu.VMEM((planes, slab, n), F32),
        pltpu.VMEM((planes, slab, n), F32),
        pltpu.VMEM((slab, n), F32),
        pltpu.VMEM((times, slab, n), F32),
        pltpu.VMEM((planes, slab, n), F32),
        pltpu.VMEM((times, rows, n), BF16),
        pltpu.VMEM((planes, tall, n), F32),
        pltpu.VMEM((planes, tall, n), F32),
    ]
    scratch += [DMA((ring,)), DMA((ring,)), DMA((6,)), DMA((6,))]
    scratch += [DMA((times,)), DMA((times,)), DMA((planes,)), DMA((planes,))]
    scratch += [DMA((ring,)), DMA((ring,)), DMA((6,)), DMA((6,))]
    scratch += [DMA((planes,)), DMA((planes,)), DMA((times,)), DMA((times,))]
    scratch += [DMA((planes,)), DMA((planes,)), DMA((planes,)), DMA((planes,))]
    return pl.pallas_call(
        functools.partial(sweep_kernel, first, last),
        out_shape=tuple(out_shape),
        in_specs=in_vmem(2),
        out_specs=tuple(in_vmem(len(out_shape))),
        scratch_shapes=scratch,
        compiler_params=pltpu.CompilerParams(
            collective_id=0 if first else 2 if last else 1,
            has_side_effects=True,
            vmem_limit_bytes=32 * 1024 * 1024,
        ),
        name="sweep_first" if first else "sweep_last" if last else "sweep",
    )(data, factors)


def regularized(gram):
    shape = gram.shape
    diagonal = lax.broadcasted_iota(jnp.int32, shape, 0) == lax.broadcasted_iota(jnp.int32, shape, 1)
    return gram + jnp.where(diagonal, RIDGE, 0.0)


def next_factors(w_ref, m_ref, ridged, a_ref, x_ref, e_ref):
    combined = m_ref[...] + RIDGE * wide(ridged, ridged)
    inverse = inverse_of(combined, a_ref, x_ref, e_ref)
    return wide(wide(w_ref[...], inverse), ridged).astype(BF16)


def solve_kernel(w_ref, m_ref, g_ref, f_ref, a_ref, x_ref, e_ref):
    f_ref[...] = next_factors(w_ref, m_ref, regularized(g_ref[...]), a_ref, x_ref, e_ref)


def solve(cross, moment, gram):
    square = pltpu.VMEM(gram.shape, F32)
    return pl.pallas_call(
        solve_kernel,
        out_shape=jax.ShapeDtypeStruct(cross.shape, BF16),
        in_specs=in_vmem(3),
        out_specs=in_vmem(1)[0],
        scratch_shapes=[square] * 3,
        compiler_params=pltpu.CompilerParams(vmem_limit_bytes=16 * 1024 * 1024),
        name="solve",
    )(cross, moment, gram)


def folded(rows):
    rows = jnp.sum(rows.reshape(rows.shape[0] // 8, 8, rows.shape[1]), axis=0)
    side = rows.shape[1] // 2
    return rows[:, :side] + rows[:, side:]


def solve_last_kernel(
    w_ref, m_ref, g_ref, p_ref, square_ref, f_ref, l_ref, sums_ref, a_ref, x_ref, e_ref
):
    ridged = regularized(g_ref[...])
    factors = next_factors(w_ref, m_ref, ridged, a_ref, x_ref, e_ref)
    f_ref[...] = factors
    inverse = inverse_of(ridged, a_ref, x_ref, e_ref)
    top = inverse.astype(BF16)
    rest = inverse - top.astype(F32)
    middle = rest.astype(BF16)
    bottom = (rest - middle.astype(F32)).astype(BF16)

    def load(k, carry):
        rows = p_ref[k]
        l_ref[k] = (narrow(rows, bottom) + narrow(rows, middle) + narrow(rows, top)).astype(BF16)
        return carry

    lax.fori_loop(0, p_ref.shape[0], load, 0)
    known = factors.astype(F32)
    quadratic = wide(wide(inverse, m_ref[...]), inverse)
    side = sums_ref.shape[1] // 2
    sums_ref[:, :side] = folded(wide(known, quadratic) * known) - 2.0 * folded(
        wide(known, inverse) * w_ref[...]
    )
    sums_ref[:, side:] = folded(square_ref[...])


def solve_last(cross, moment, gram, projection, squares):
    square = pltpu.VMEM(gram.shape, F32)
    return pl.pallas_call(
        solve_last_kernel,
        out_shape=(
            jax.ShapeDtypeStruct(cross.shape, BF16),
            jax.ShapeDtypeStruct(projection.shape, BF16),
            jax.ShapeDtypeStruct(squares.shape, F32),
        ),
        in_specs=in_vmem(5),
        out_specs=tuple(in_vmem(3)),
        scratch_shapes=[square] * 3,
        compiler_params=pltpu.CompilerParams(vmem_limit_bytes=16 * 1024 * 1024),
        name="solve_last",
    )(cross, moment, gram, projection, squares)


def tail_kernel(
    f_ref, own_ref, all_ref, lag_ref, base_ref, earlier_ref, sums_ref,
    fbuf, before, lag, base, message, message_in, message_all,
    f_s, f_r, row_s, row_r, ta_s, ta_r, tb_s, tb_r,
):
    me = Place()
    span, n = all_ref.shape
    edge = before.shape[0]
    me.greet(me.time_others() + me.plane_others())
    me.share_plane(f_ref, fbuf, f_s, f_r)
    fbuf[me.p] = f_ref[...]
    me.finish_plane(f_ref, fbuf, f_s, f_r)
    following = lax.rem(me.t + 1, me.times)
    last_rows = fbuf.at[me.planes - 1, pl.ds(fbuf.shape[1] - edge, edge)]
    row = me.copy(last_rows, before, row_s, row_r, t=following)
    row.start()
    factors = fbuf[...].reshape(span, n)
    all_ref[...] = factors
    rolled = pltpu.roll(factors.astype(F32), 1, 0)
    first = lax.broadcasted_iota(jnp.int32, (span, n), 0) == 0
    row.wait()
    head = before[...].astype(F32)[edge - 1 :, :]
    head = head * jnp.where(me.t == 0, 0.0, 1.0)
    earlier = jnp.where(first, head, rolled).astype(BF16)
    earlier_ref[...] = earlier
    lag[...] = column_gram(factors, earlier)
    base[...] = column_gram(earlier, earlier)
    slab = n // me.planes
    here = pl.ds(pl.multiple_of(me.p * slab, slab), slab)
    message[:slab, :] = lag[here, :]
    message[slab : 2 * slab, :] = base[here, :]
    message[2 * slab :, :] = own_ref[...]
    me.share_times(message, message_in, ta_s, ta_r)
    message_in[me.t] = message[...]
    me.finish_times(message, message_in, ta_s, ta_r)
    message_all[me.p] = total_of(message_in)
    me.share_plane(message_all.at[me.p], message_all, tb_s, tb_r)
    me.finish_plane(message_all.at[me.p], message_all, tb_s, tb_r)
    lag_ref[...] = message_all[:, :slab, :].reshape(n, n)
    base_ref[...] = message_all[:, slab : 2 * slab, :].reshape(n, n)
    sums_ref[...] = total_of(message_all[:, 2 * slab :, :])


def tail(factors, own):
    planes, times = lax.axis_size("series"), lax.axis_size("tm")
    slab, n = factors.shape
    span = slab * planes
    tall = 2 * (n // planes) + own.shape[0]
    square = jax.ShapeDtypeStruct((n, n), F32)
    block = jax.ShapeDtypeStruct((span, n), BF16)
    return pl.pallas_call(
        tail_kernel,
        out_shape=(block, square, square, block, jax.ShapeDtypeStruct(own.shape, F32)),
        in_specs=in_vmem(2),
        out_specs=tuple(in_vmem(5)),
        scratch_shapes=[
            pltpu.VMEM((planes, slab, n), BF16),
            pltpu.VMEM((16, n), BF16),
            pltpu.VMEM((n, n), F32),
            pltpu.VMEM((n, n), F32),
            pltpu.VMEM((tall, n), F32),
            pltpu.VMEM((times, tall, n), F32),
            pltpu.VMEM((planes, tall, n), F32),
            DMA((planes,)), DMA((planes,)), DMA, DMA,
            DMA((times,)), DMA((times,)), DMA((planes,)), DMA((planes,)),
        ],
        compiler_params=pltpu.CompilerParams(
            collective_id=3, has_side_effects=True, vmem_limit_bytes=32 * 1024 * 1024
        ),
        name="tail",
    )(factors, own)


def fit_kernel(
    lag_ref, base_ref, f_ref, earlier_ref, sums_ref,
    move_ref, news_ref, factors_ref, share_ref, a_ref, x_ref, e_ref,
):
    inverse = inverse_of(regularized(base_ref[...]), a_ref, x_ref, e_ref)
    move = wide(lag_ref[...], inverse)
    move_ref[...] = move
    predicted = lax.dot_general(
        earlier_ref[...].astype(F32),
        move,
        (((1,), (1,)), ((), ())),
        precision=lax.Precision.HIGHEST,
        preferred_element_type=F32,
    )
    news_ref[...] = f_ref[...].astype(F32) - predicted
    factors_ref[...] = f_ref[...]
    side = sums_ref.shape[1] // 2
    total = jnp.sum(sums_ref[:, side:])
    share_ref[0, 0] = (total + jnp.sum(sums_ref[:, :side])) / total


def fit(lagged, base, factors, earlier, sums):
    span, n = factors.shape
    square = pltpu.VMEM((n, n), F32)
    return pl.pallas_call(
        fit_kernel,
        out_shape=(
            jax.ShapeDtypeStruct((n, n), F32),
            jax.ShapeDtypeStruct((span, n), F32),
            jax.ShapeDtypeStruct((span, n), BF16),
            jax.ShapeDtypeStruct((1, 1), F32),
        ),
        in_specs=in_vmem(5),
        out_specs=(*in_vmem(3), pl.BlockSpec(memory_space=pltpu.SMEM)),
        scratch_shapes=[square] * 3,
        compiler_params=pltpu.CompilerParams(vmem_limit_bytes=16 * 1024 * 1024),
        name="fit",
    )(lagged, base, factors, earlier, sums)


def body(data, factors_init):
    factors = factors_init
    for step in range(ITERS):
        first, last = step == 0, step == ITERS - 1
        cross, moment, gram, *extra = sweep(data, factors, first, last)
        if not last:
            factors = solve(cross, moment, gram)
    projection, squares = extra
    factors, loadings, own = solve_last(cross, moment, gram, projection, squares)
    loadings = loadings.reshape(data.shape[0], factors.shape[1])
    gathered, lagged, base, earlier, sums = tail(factors, own)
    transition, innovations, factors, share = fit(lagged, base, gathered, earlier, sums)
    return (loadings, factors, innovations, transition, share.reshape(()))


def solution(mesh):
    return jax.shard_map(
        body,
        mesh=mesh,
        in_specs=(P("series", "tm"), P("tm", None)),
        out_specs=(P("series", None), P("tm", None), P("tm", None), P(), P()),
        check_vma=False,
    )
```

time: 269 us -> 251 us (0.933)
  Pallas kernels: 261 us -> 248 us
    pallas_call x13 -> x7, Pallas kernels: 255 us -> 241 us  [the longest x3 145 us: sweep(): pl.pallas_call(functools.partial(sweep_kernel, first, last), out_shape=tu...]
    unnamed x7 -> x4, local copies, waits for them, and re-layouts: 5.4 us -> 3.13 us
where the time goes in v2:
time: 251 us; the launch traced here: 252 us
  Pallas kernels  248 us (99%)
  local copies, waits for them, and re-layouts  3.13 us (1%)
    pallas_call x3, Pallas kernels, sweep(): pl.pallas_call(functools.partial(sweep_kernel, first, last), out_shape=tu...  145 us
    pallas_call x1, Pallas kernels, solve_last(): pl.pallas_call(solve_last_kernel, out_shape=(jax.ShapeDtypeStruct(cross.s...  35.6 us
    pallas_call x2, Pallas kernels, solve(): pl.pallas_call(solve_kernel, out_shape=jax.ShapeDtypeStruct(cross.shape,...  32.1 us
    pallas_call x1, Pallas kernels, tail(): pl.pallas_call(tail_kernel, out_shape=(block, square, square, block, jax....  28.5 us
    pallas_call x1, Pallas kernels, fit(): pl.pallas_call(fit_kernel, out_shape=(jax.ShapeDtypeStruct((n, n), F32),...  6.56 us

profile of v2, /device:TPU:1, one launch (start us, length us, event | category | flops | bytes accessed | tf_op | source)
XLA Modules:
  0.0 251.8 jit_solution(11594535019373001513)
XLA Ops:
  0.6 0.0 copy-start
  0.6 2.2 copy-done
  2.8 0.0 copy-start.1
  2.8 0.9 copy-done.1
  3.8 46.2 %sweep_first.1 = (f32[32,256]{1,0:T(8,128)S(1)}, f32[256,256]{1,0:T(8,128)S(1)}, f32[256,256]{1,0:T(8,128)S(1)}) custom-call(bf16[4096,512]{1,0:T(8,128)(2,1)S(1)} %copy-done, bf16[512,256]{1,0:T(8,128)(2,1)S(1)} %copy-done.1), custom_call_target="tpu_custom_call" | custom-call | tf_op jit(solution)/shard_map/sweep_first/pallas_call | solution.py:436
  50.0 6.1 %solve.2.refs_1_ = bf16[32,256]{1,0:T(8,128)(2,1)S(1)} custom-call(f32[32,256]{1,0:T(8,128)S(1)} %get-tuple-element.28.w_ref, f32[256,256]{1,0:T(8,128)S(1)} %get-tuple-element.29.m_ref, f32[256,256]{1,0:T(8,128)S(1)} %get-tuple-element.30.g_ref), custom_call_target="tpu_custom_call" | custom-call | tf_op jit(solution)/shard_map/solve/pallas_call | solution.py:469
  56.0 49.8 %sweep.1 = (f32[32,256]{1,0:T(8,128)S(1)}, f32[256,256]{1,0:T(8,128)S(1)}, f32[256,256]{1,0:T(8,128)S(1)}) custom-call(bf16[4096,512]{1,0:T(8,128)(2,1)S(1)} %copy-done, bf16[32,256]{1,0:T(8,128)(2,1)S(1)} %solve.2.refs_1_), custom_call_target="tpu_custom_call" | custom-call | tf_op jit(solution)/shard_map/sweep/pallas_call | solution.py:436
  105.8 26.1 %solve.3.refs_1_ = bf16[32,256]{1,0:T(8,128)(2,1)S(1)} custom-call(f32[32,256]{1,0:T(8,128)S(1)} %get-tuple-element.31.w_ref, f32[256,256]{1,0:T(8,128)S(1)} %get-tuple-element.32.m_ref, f32[256,256]{1,0:T(8,128)S(1)} %get-tuple-element.33.g_ref), custom_call_target="tpu_custom_call" | custom-call | tf_op jit(solution)/shard_map/solve/pallas_call | solution.py:469
  131.9 49.0 %sweep_last.1 = (f32[32,256]{1,0:T(8,128)S(1)}, f32[256,256]{1,0:T(8,128)S(1)}, f32[256,256]{1,0:T(8,128)S(1)}, bf16[8,512,256]{2,1,0:T(8,128)(2,1)S(1)}, f32[8,256]{1,0:T(8,128)S(1)}) custom-call(bf16[4096,512]{1,0:T(8,128)(2,1)S(1)} %copy-done, bf16[32,256]{1,0:T(8,128)(2,1)S(1)} %solve.3.refs_1_), custom_call_target="tpu_custom_call" | custom-call | tf_op jit(solution)/shard_map/sweep_last/pallas_call | solution.py:436
  180.9 35.6 %solve_last.1 = (bf16[32,256]{1,0:T(8,128)(2,1)S(1)}, bf16[8,512,256]{2,1,0:T(8,128)(2,1)}, f32[8,256]{1,0:T(8,128)S(1)}) custom-call(f32[32,256]{1,0:T(8,128)S(1)} %get-tuple-element.34.w_ref, f32[256,256]{1,0:T(8,128)S(1)} %get-tuple-element.35.m_ref, f32[256,256]{1,0:T(8,128)S(1)} %get-tuple-element.36.g_ref, ...), custom_call_target="tpu_custom_call" | custom-call | tf_op jit(solution)/shard_map/solve_last/pallas_call | solution.py:515
  216.6 28.5 %tail.1 = (bf16[512,256]{1,0:T(8,128)(2,1)S(1)}, f32[256,256]{1,0:T(8,128)S(1)}, f32[256,256]{1,0:T(8,128)S(1)}, bf16[512,256]{1,0:T(8,128)(2,1)S(1)}, f32[8,256]{1,0:T(8,128)S(1)}) custom-call(bf16[32,256]{1,0:T(8,128)(2,1)S(1)} %get-tuple-element.40.f_ref, f32[8,256]{1,0:T(8,128)S(1)} %get-tuple-element.41.own_ref), custom_call_target="tpu_custom_call" | custom-call | tf_op jit(solution)/shard_map/tail/pallas_call | solution.py:580
  245.0 6.6 %fit.1 = (f32[256,256]{1,0:T(8,128)}, f32[512,256]{1,0:T(8,128)}, bf16[512,256]{1,0:T(8,128)(2,1)}, f32[1,1]{1,0:T(1,128)}) custom-call(f32[256,256]{1,0:T(8,128)S(1)} %get-tuple-element.42.lag_ref, f32[256,256]{1,0:T(8,128)S(1)} %get-tuple-element.43.base_ref, bf16[512,256]{1,0:T(8,128)(2,1)S(1)} %get-tuple-element.44.f_ref, ...), custom_call_target="tpu_custom_call" | custom-call | tf_op jit(solution)/shard_map/fit/pallas_call | solution.py:627
Async XLA Ops:
  0.6 2.2 copy-start
  2.8 0.9 copy-start.1

commit v3 on v2

--- a/solution.py
+++ b/solution.py
@@ -27,31 +27,35 @@
     return lax.dot_general(left, right, (((0,), (0,)), ((), ())), preferred_element_type=F32)
 
 
-def inverse_of(gram, a_ref, x_ref, e_ref):
-    n = gram.shape[0]
+def inverses_of(grams, a_ref, x_ref, e_ref):
+    n = grams[0].shape[0]
+    each = range(len(grams))
     rows = lax.broadcasted_iota(jnp.int32, (n, n), 0)
     cols = lax.broadcasted_iota(jnp.int32, (n, n), 1)
     diagonal = rows == cols
-    masked = jnp.where(diagonal, gram, 0.0)
-    down = lax.rsqrt(jnp.sum(masked, axis=1, keepdims=True))
-    across = lax.rsqrt(jnp.sum(masked, axis=0, keepdims=True))
-    scaled = gram * down * across
-    a_ref[...] = scaled
-    bound = jnp.max(jnp.sum(jnp.abs(scaled), axis=0, keepdims=True))
-    alpha = 1.9 / bound
-    start = jnp.where(diagonal, alpha, 0.0)
-    x_ref[...] = start
-    e_ref[...] = jnp.where(diagonal, 1.0, 0.0) - alpha * scaled
+    down, across, alpha = [], [], []
+    for i in each:
+        masked = jnp.where(diagonal, grams[i], 0.0)
+        down.append(lax.rsqrt(jnp.sum(masked, axis=1, keepdims=True)))
+        across.append(lax.rsqrt(jnp.sum(masked, axis=0, keepdims=True)))
+        scaled = grams[i] * down[i] * across[i]
+        a_ref[i] = scaled
+        alpha.append(1.9 / jnp.max(jnp.sum(jnp.abs(scaled), axis=0, keepdims=True)))
+        x_ref[i] = jnp.where(diagonal, alpha[i], 0.0)
+        e_ref[i] = jnp.where(diagonal, 1.0, 0.0) - alpha[i] * scaled
+
+    def worst_of(values):
+        return functools.reduce(jnp.maximum, values)
 
     def squaring(carry):
         step, _ = carry
         for _ in range(2):
-            error = e_ref[...]
-            guess = x_ref[...]
-            e_ref[...] = narrow(error, error)
-            x_ref[...] = guess + narrow(guess, error)
-        final = e_ref[...]
-        return step + 1, jnp.sum(final * final)
+            for i in each:
+                error = e_ref[i]
+                guess = x_ref[i]
+                e_ref[i] = narrow(error, error)
+                x_ref[i] = guess + narrow(guess, error)
+        return step + 1, worst_of([jnp.sum(e_ref[i] * e_ref[i]) for i in each])
 
     lax.while_loop(
         lambda c: jnp.logical_and(c[0] < 10, jnp.logical_and(c[1] > 1e-2, c[1] < 1e3)),
@@ -60,15 +64,16 @@
     )
 
     def residual():
-        error = jnp.where(diagonal, 1.0, 0.0) - wide(a_ref[...], x_ref[...])
-        e_ref[...] = error
-        return jnp.max(jnp.abs(error))
+        for i in each:
+            e_ref[i] = jnp.where(diagonal, 1.0, 0.0) - wide(a_ref[i], x_ref[i])
+        return worst_of([jnp.max(jnp.abs(e_ref[i])) for i in each])
 
     def refine(carry):
         step, _ = carry
         worst = residual()
-        guess = x_ref[...]
-        x_ref[...] = guess + narrow(guess, e_ref[...])
+        for i in each:
+            guess = x_ref[i]
+            x_ref[i] = guess + narrow(guess, e_ref[i])
         return step + 1, worst
 
     _, worst = lax.while_loop(
@@ -79,13 +84,15 @@
 
     @pl.when(worst >= 5e-4)
     def _():
-        x_ref[...] = jnp.where(diagonal, alpha, 0.0)
+        for i in each:
+            x_ref[i] = jnp.where(diagonal, alpha[i], 0.0)
 
         def newton(carry):
             step, _ = carry
             error = residual()
-            guess = x_ref[...]
-            x_ref[...] = guess + wide(guess, e_ref[...])
+            for i in each:
+                guess = x_ref[i]
+                x_ref[i] = guess + wide(guess, e_ref[i])
             return step + 1, error
 
         lax.while_loop(
@@ -94,7 +101,11 @@
             (0, jnp.float32(1.0)),
         )
 
-    return x_ref[...] * down * across
+    return [x_ref[i] * down[i] * across[i] for i in each]
+
+
+def squares_of(count, n):
+    return [pltpu.VMEM((count, n, n), F32)] * 3
 
 
 class Place:
@@ -124,10 +135,12 @@
             device_id_type=MESH,
         )
 
-    def greet(self, others):
+    def greet(self, others, meanwhile=None):
         barrier = pltpu.get_barrier_semaphore()
         for p, t in others:
             pl.semaphore_signal(barrier, inc=1, device_id=(p, t), device_id_type=MESH)
+        if meanwhile is not None:
+            meanwhile()
         pl.semaphore_wait(barrier, len(others))
 
     def plane_others(self):
@@ -206,7 +219,10 @@
     x_ref, f_ref, w_ref, m_ref, g_ref = take(5)
     if last:
         all_ref, square_ref = take(2)
-    if not first:
+    if first:
+        x_from = x_ref
+        x_ref, x_sem = take(2)
+    else:
         fbuf, f_s, f_r = take(3)
     part, other, chip, acc, relay_in, direct_in, relay_out, joined_in = take(8)
     gram, gram_in, gram_all, moment, moment_in, moment_own, moment_times, moment_all = take(8)
@@ -221,7 +237,14 @@
     up, down, far = me.ring_at(1), me.ring_at(ring - 1), me.ring_at(2)
     t_up, t_down, t_far = me.time_of(up), me.time_of(down), me.time_of(far)
     slab = gram_in.shape[1]
-    me.greet(me.time_others() + me.plane_others())
+
+    def bring():
+        x_copy = pltpu.make_async_copy(x_from, x_ref, x_sem)
+        x_copy.start()
+        gram[...] = column_gram(f_ref[...], f_ref[...])
+        x_copy.wait()
+
+    me.greet(me.time_others() + me.plane_others(), bring if first else None)
 
     if first:
         def factors():
@@ -234,7 +257,8 @@
         def factors():
             return fbuf[...].reshape(x_ref.shape[1], f_ref.shape[1])
 
-    gram[...] = column_gram(factors(), factors())
+    if not first:
+        gram[...] = column_gram(factors(), factors())
     mine = gram.at[pl.ds(pl.multiple_of(me.p * slab, slab), slab)]
     me.share_times(mine, gram_in, ga_s, ga_r)
     gram_in[me.t] = mine[...]
@@ -411,7 +435,10 @@
             jax.ShapeDtypeStruct((8, n), F32),
         ]
     scratch = []
-    if not first:
+    if first:
+        out_shape += [jax.ShapeDtypeStruct(data.shape, BF16)]
+        scratch += [DMA]
+    else:
         scratch += [pltpu.VMEM((planes, tall, n), BF16), DMA((planes,)), DMA((planes,))]
     scratch += [pltpu.VMEM((ring, rows, n), BF16)] * 3 + [pltpu.VMEM((ring, rows, n), F32)]
     scratch += [pltpu.VMEM((2, half, n), BF16)] * 4
@@ -436,13 +463,13 @@
     return pl.pallas_call(
         functools.partial(sweep_kernel, first, last),
         out_shape=tuple(out_shape),
-        in_specs=in_vmem(2),
+        in_specs=[pl.BlockSpec(memory_space=pltpu.HBM if first else pltpu.VMEM), *in_vmem(1)],
         out_specs=tuple(in_vmem(len(out_shape))),
         scratch_shapes=scratch,
         compiler_params=pltpu.CompilerParams(
             collective_id=0 if first else 2 if last else 1,
             has_side_effects=True,
-            vmem_limit_bytes=32 * 1024 * 1024,
+            vmem_limit_bytes=(48 if first else 32) * 1024 * 1024,
         ),
         name="sweep_first" if first else "sweep_last" if last else "sweep",
     )(data, factors)
@@ -454,26 +481,34 @@
     return gram + jnp.where(diagonal, RIDGE, 0.0)
 
 
-def next_factors(w_ref, m_ref, ridged, a_ref, x_ref, e_ref):
+def next_factors(w_ref, inverse, ridged):
+    return wide(wide(w_ref[...], inverse), ridged).astype(BF16)
+
+
+def solve_kernel(w_ref, m_ref, g_ref, f_ref, *state):
+    ridged = regularized(g_ref[...])
+    (inverse,) = inverses_of([m_ref[...] + RIDGE * wide(ridged, ridged)], *state)
+    f_ref[...] = next_factors(w_ref, inverse, ridged)
+
+
+def solve_last_kernel(w_ref, m_ref, g_ref, f_ref, inverse_ref, *state):
+    ridged = regularized(g_ref[...])
     combined = m_ref[...] + RIDGE * wide(ridged, ridged)
-    inverse = inverse_of(combined, a_ref, x_ref, e_ref)
-    return wide(wide(w_ref[...], inverse), ridged).astype(BF16)
-
-
-def solve_kernel(w_ref, m_ref, g_ref, f_ref, a_ref, x_ref, e_ref):
-    f_ref[...] = next_factors(w_ref, m_ref, regularized(g_ref[...]), a_ref, x_ref, e_ref)
-
-
-def solve(cross, moment, gram):
-    square = pltpu.VMEM(gram.shape, F32)
+    inverse, inverse_ref[...] = inverses_of([combined, ridged], *state)
+    f_ref[...] = next_factors(w_ref, inverse, ridged)
+
+
+def solve(cross, moment, gram, last):
+    factors = jax.ShapeDtypeStruct(cross.shape, BF16)
+    square = jax.ShapeDtypeStruct(gram.shape, F32)
     return pl.pallas_call(
-        solve_kernel,
-        out_shape=jax.ShapeDtypeStruct(cross.shape, BF16),
+        solve_last_kernel if last else solve_kernel,
+        out_shape=(factors, square) if last else (factors,),
         in_specs=in_vmem(3),
-        out_specs=in_vmem(1)[0],
-        scratch_shapes=[square] * 3,
+        out_specs=tuple(in_vmem(2 if last else 1)),
+        scratch_shapes=squares_of(2 if last else 1, gram.shape[0]),
         compiler_params=pltpu.CompilerParams(vmem_limit_bytes=16 * 1024 * 1024),
-        name="solve",
+        name="solve_last" if last else "solve",
     )(cross, moment, gram)
 
 
@@ -483,53 +518,10 @@
     return rows[:, :side] + rows[:, side:]
 
 
-def solve_last_kernel(
-    w_ref, m_ref, g_ref, p_ref, square_ref, f_ref, l_ref, sums_ref, a_ref, x_ref, e_ref
-):
-    ridged = regularized(g_ref[...])
-    factors = next_factors(w_ref, m_ref, ridged, a_ref, x_ref, e_ref)
-    f_ref[...] = factors
-    inverse = inverse_of(ridged, a_ref, x_ref, e_ref)
-    top = inverse.astype(BF16)
-    rest = inverse - top.astype(F32)
-    middle = rest.astype(BF16)
-    bottom = (rest - middle.astype(F32)).astype(BF16)
-
-    def load(k, carry):
-        rows = p_ref[k]
-        l_ref[k] = (narrow(rows, bottom) + narrow(rows, middle) + narrow(rows, top)).astype(BF16)
-        return carry
-
-    lax.fori_loop(0, p_ref.shape[0], load, 0)
-    known = factors.astype(F32)
-    quadratic = wide(wide(inverse, m_ref[...]), inverse)
-    side = sums_ref.shape[1] // 2
-    sums_ref[:, :side] = folded(wide(known, quadratic) * known) - 2.0 * folded(
-        wide(known, inverse) * w_ref[...]
-    )
-    sums_ref[:, side:] = folded(square_ref[...])
-
-
-def solve_last(cross, moment, gram, projection, squares):
-    square = pltpu.VMEM(gram.shape, F32)
-    return pl.pallas_call(
-        solve_last_kernel,
-        out_shape=(
-            jax.ShapeDtypeStruct(cross.shape, BF16),
-            jax.ShapeDtypeStruct(projection.shape, BF16),
-            jax.ShapeDtypeStruct(squares.shape, F32),
-        ),
-        in_specs=in_vmem(5),
-        out_specs=tuple(in_vmem(3)),
-        scratch_shapes=[square] * 3,
-        compiler_params=pltpu.CompilerParams(vmem_limit_bytes=16 * 1024 * 1024),
-        name="solve_last",
-    )(cross, moment, gram, projection, squares)
-
-
 def tail_kernel(
-    f_ref, own_ref, all_ref, lag_ref, base_ref, earlier_ref, sums_ref,
-    fbuf, before, lag, base, message, message_in, message_all,
+    f_ref, w_ref, m_ref, inverse_ref, p_ref, square_ref,
+    all_ref, lag_ref, base_ref, earlier_ref, sums_ref, l_ref,
+    top, middle, bottom, fbuf, before, lag, base, message, message_in, message_all,
     f_s, f_r, row_s, row_r, ta_s, ta_r, tb_s, tb_r,
 ):
     me = Place()
@@ -538,6 +530,29 @@
     me.greet(me.time_others() + me.plane_others())
     me.share_plane(f_ref, fbuf, f_s, f_r)
     fbuf[me.p] = f_ref[...]
+    slab = n // me.planes
+
+    inverse = inverse_ref[...]
+    known = f_ref[...].astype(F32)
+    quadratic = wide(wide(inverse, m_ref[...]), inverse)
+    side = n // 2
+    message[2 * slab :, :side] = folded(wide(known, quadratic) * known) - 2.0 * folded(
+        wide(known, inverse) * w_ref[...]
+    )
+    message[2 * slab :, side:] = folded(square_ref[...])
+    top[...] = inverse.astype(BF16)
+    rest = inverse - top[...].astype(F32)
+    middle[...] = rest.astype(BF16)
+    bottom[...] = (rest - middle[...].astype(F32)).astype(BF16)
+
+    def load(k, carry):
+        rows = p_ref[k]
+        parts = narrow(rows, bottom[...]) + narrow(rows, middle[...]) + narrow(rows, top[...])
+        l_ref[k] = parts.astype(BF16)
+        return carry
+
+    count = p_ref.shape[0]
+    lax.fori_loop(0, count // 4, load, 0)
     me.finish_plane(f_ref, fbuf, f_s, f_r)
     following = lax.rem(me.t + 1, me.times)
     last_rows = fbuf.at[me.planes - 1, pl.ds(fbuf.shape[1] - edge, edge)]
@@ -554,35 +569,41 @@
     earlier_ref[...] = earlier
     lag[...] = column_gram(factors, earlier)
     base[...] = column_gram(earlier, earlier)
-    slab = n // me.planes
     here = pl.ds(pl.multiple_of(me.p * slab, slab), slab)
     message[:slab, :] = lag[here, :]
     message[slab : 2 * slab, :] = base[here, :]
-    message[2 * slab :, :] = own_ref[...]
     me.share_times(message, message_in, ta_s, ta_r)
     message_in[me.t] = message[...]
+    lax.fori_loop(count // 4, count // 2, load, 0)
     me.finish_times(message, message_in, ta_s, ta_r)
     message_all[me.p] = total_of(message_in)
     me.share_plane(message_all.at[me.p], message_all, tb_s, tb_r)
+    lax.fori_loop(count // 2, count, load, 0)
     me.finish_plane(message_all.at[me.p], message_all, tb_s, tb_r)
     lag_ref[...] = message_all[:, :slab, :].reshape(n, n)
     base_ref[...] = message_all[:, slab : 2 * slab, :].reshape(n, n)
     sums_ref[...] = total_of(message_all[:, 2 * slab :, :])
 
 
-def tail(factors, own):
+def tail(factors, cross, moment, inverse, projection, squares):
     planes, times = lax.axis_size("series"), lax.axis_size("tm")
     slab, n = factors.shape
     span = slab * planes
-    tall = 2 * (n // planes) + own.shape[0]
+    tall = 2 * (n // planes) + squares.shape[0]
     square = jax.ShapeDtypeStruct((n, n), F32)
     block = jax.ShapeDtypeStruct((span, n), BF16)
+    sums = jax.ShapeDtypeStruct(squares.shape, F32)
     return pl.pallas_call(
         tail_kernel,
-        out_shape=(block, square, square, block, jax.ShapeDtypeStruct(own.shape, F32)),
-        in_specs=in_vmem(2),
-        out_specs=tuple(in_vmem(5)),
+        out_shape=(
+            block, square, square, block, sums, jax.ShapeDtypeStruct(projection.shape, BF16)
+        ),
+        in_specs=in_vmem(6),
+        out_specs=tuple(in_vmem(6)),
         scratch_shapes=[
+            pltpu.VMEM((n, n), BF16),
+            pltpu.VMEM((n, n), BF16),
+            pltpu.VMEM((n, n), BF16),
             pltpu.VMEM((planes, slab, n), BF16),
             pltpu.VMEM((16, n), BF16),
             pltpu.VMEM((n, n), F32),
@@ -597,14 +618,16 @@
             collective_id=3, has_side_effects=True, vmem_limit_bytes=32 * 1024 * 1024
         ),
         name="tail",
-    )(factors, own)
+    )(factors, cross, moment, inverse, projection, squares)
 
 
 def fit_kernel(
-    lag_ref, base_ref, f_ref, earlier_ref, sums_ref,
-    move_ref, news_ref, factors_ref, share_ref, a_ref, x_ref, e_ref,
+    lag_ref, base_ref, f_ref, earlier_ref, sums_ref, l_ref,
+    move_ref, news_ref, factors_ref, share_ref, loadings_ref, a_ref, x_ref, e_ref, sem,
 ):
-    inverse = inverse_of(regularized(base_ref[...]), a_ref, x_ref, e_ref)
+    saved = pltpu.make_async_copy(l_ref, loadings_ref, sem)
+    saved.start()
+    (inverse,) = inverses_of([regularized(base_ref[...])], a_ref, x_ref, e_ref)
     move = wide(lag_ref[...], inverse)
     move_ref[...] = move
     predicted = lax.dot_general(
@@ -619,11 +642,11 @@
     side = sums_ref.shape[1] // 2
     total = jnp.sum(sums_ref[:, side:])
     share_ref[0, 0] = (total + jnp.sum(sums_ref[:, :side])) / total
-
-
-def fit(lagged, base, factors, earlier, sums):
+    saved.wait()
+
+
+def fit(lagged, base, factors, earlier, sums, loadings):
     span, n = factors.shape
-    square = pltpu.VMEM((n, n), F32)
     return pl.pallas_call(
         fit_kernel,
         out_shape=(
@@ -631,27 +654,36 @@
             jax.ShapeDtypeStruct((span, n), F32),
             jax.ShapeDtypeStruct((span, n), BF16),
             jax.ShapeDtypeStruct((1, 1), F32),
+            jax.ShapeDtypeStruct(loadings.shape, BF16),
         ),
-        in_specs=in_vmem(5),
-        out_specs=(*in_vmem(3), pl.BlockSpec(memory_space=pltpu.SMEM)),
-        scratch_shapes=[square] * 3,
+        in_specs=in_vmem(6),
+        out_specs=(
+            *in_vmem(3),
+            pl.BlockSpec(memory_space=pltpu.SMEM),
+            pl.BlockSpec(memory_space=pltpu.HBM),
+        ),
+        scratch_shapes=squares_of(1, n) + [DMA],
         compiler_params=pltpu.CompilerParams(vmem_limit_bytes=16 * 1024 * 1024),
         name="fit",
-    )(lagged, base, factors, earlier, sums)
+    )(lagged, base, factors, earlier, sums, loadings)
 
 
 def body(data, factors_init):
-    factors = factors_init
+    factors, held = factors_init, data
     for step in range(ITERS):
         first, last = step == 0, step == ITERS - 1
-        cross, moment, gram, *extra = sweep(data, factors, first, last)
-        if not last:
-            factors = solve(cross, moment, gram)
+        cross, moment, gram, *extra = sweep(held, factors, first, last)
+        if first:
+            (held,) = extra
+        factors, *inverse = solve(cross, moment, gram, last)
     projection, squares = extra
-    factors, loadings, own = solve_last(cross, moment, gram, projection, squares)
+    gathered, lagged, base, earlier, sums, loadings = tail(
+        factors, cross, moment, *inverse, projection, squares
+    )
+    transition, innovations, factors, share, loadings = fit(
+        lagged, base, gathered, earlier, sums, loadings
+    )
     loadings = loadings.reshape(data.shape[0], factors.shape[1])
-    gathered, lagged, base, earlier, sums = tail(factors, own)
-    transition, innovations, factors, share = fit(lagged, base, gathered, earlier, sums)
     return (loadings, factors, innovations, transition, share.reshape(()))
 
 

time: 251 us -> 245 us (0.976)
  Pallas kernels: 248 us -> 242 us
    pallas_call x4, Pallas kernels: 96.3 us -> 90.1 us  [the longest x3 61.7 us: solve(): pl.pallas_call(solve_last_kernel if last else solve_kernel, out_shape=(fa...]
where the time goes in v3:
time: 245 us; the launch traced here: 244 us
  Pallas kernels  242 us (99%)
    pallas_call x3, Pallas kernels, sweep(): pl.pallas_call(functools.partial(sweep_kernel, first, last), out_shape=tu...  145 us
    pallas_call x3, Pallas kernels, solve(): pl.pallas_call(solve_last_kernel if last else solve_kernel, out_shape=(fa...  61.7 us
    pallas_call x1, Pallas kernels, tail(): pl.pallas_call(tail_kernel, out_shape=(block, square, square, block, sums...  28.4 us
    pallas_call x1, Pallas kernels, fit(): pl.pallas_call(fit_kernel, out_shape=(jax.ShapeDtypeStruct((n, n), F32),...  7.2 us

profile of v3, /device:TPU:1, one launch (start us, length us, event | category | flops | bytes accessed | tf_op | source)
XLA Modules:
  0.0 243.7 jit_solution(6561024877955582412)
XLA Ops:
  0.6 0.0 copy-start
  0.6 0.9 copy-done
  1.6 45.8 %sweep_first.1 = (f32[32,256]{1,0:T(8,128)S(1)}, f32[256,256]{1,0:T(8,128)S(1)}, f32[256,256]{1,0:T(8,128)S(1)}, bf16[4096,512]{1,0:T(8,128)(2,1)S(1)}) custom-call(bf16[4096,512]{1,0:T(8,128)(2,1)} %refs_0_.1, bf16[512,256]{1,0:T(8,128)(2,1)S(1)} %copy-done), custom_call_target="tpu_custom_call" | custom-call | tf_op jit(solution)/shard_map/sweep_first/pallas_call | solution.py:463
  47.4 6.7 %solve.2.refs_1_ = bf16[32,256]{1,0:T(8,128)(2,1)S(1)} custom-call(f32[32,256]{1,0:T(8,128)S(1)} %get-tuple-element.31.w_ref, f32[256,256]{1,0:T(8,128)S(1)} %get-tuple-element.32.m_ref, f32[256,256]{1,0:T(8,128)S(1)} %get-tuple-element.33.g_ref), custom_call_target="tpu_custom_call" | custom-call | tf_op jit(solution)/shard_map/solve/pallas_call | solution.py:504
  54.1 49.8 %sweep.1 = (f32[32,256]{1,0:T(8,128)S(1)}, f32[256,256]{1,0:T(8,128)S(1)}, f32[256,256]{1,0:T(8,128)S(1)}) custom-call(bf16[4096,512]{1,0:T(8,128)(2,1)S(1)} %get-tuple-element.30.refs_0_, bf16[32,256]{1,0:T(8,128)(2,1)S(1)} %solve.2.refs_1_), custom_call_target="tpu_custom_call" | custom-call | tf_op jit(solution)/shard_map/sweep/pallas_call | solution.py:463
  103.9 26.1 %solve.3.refs_1_ = bf16[32,256]{1,0:T(8,128)(2,1)S(1)} custom-call(f32[32,256]{1,0:T(8,128)S(1)} %get-tuple-element.34.w_ref, f32[256,256]{1,0:T(8,128)S(1)} %get-tuple-element.35.m_ref, f32[256,256]{1,0:T(8,128)S(1)} %get-tuple-element.36.g_ref), custom_call_target="tpu_custom_call" | custom-call | tf_op jit(solution)/shard_map/solve/pallas_call | solution.py:504
  130.0 49.0 %sweep_last.1 = (f32[32,256]{1,0:T(8,128)S(1)}, f32[256,256]{1,0:T(8,128)S(1)}, f32[256,256]{1,0:T(8,128)S(1)}, bf16[8,512,256]{2,1,0:T(8,128)(2,1)S(1)}, f32[8,256]{1,0:T(8,128)S(1)}) custom-call(bf16[4096,512]{1,0:T(8,128)(2,1)S(1)} %get-tuple-element.30.refs_0_, bf16[32,256]{1,0:T(8,128)(2,1)S(1)} %solve.3.refs_1_), custom_call_target="tpu_custom_call" | custom-call | tf_op jit(solution)/shard_map/sweep_last/pallas_call | solution.py:463
  179.0 28.9 %solve_last.1 = (bf16[32,256]{1,0:T(8,128)(2,1)S(1)}, f32[256,256]{1,0:T(8,128)S(1)}) custom-call(f32[32,256]{1,0:T(8,128)S(1)} %get-tuple-element.37.w_ref, f32[256,256]{1,0:T(8,128)S(1)} %get-tuple-element.38.m_ref, f32[256,256]{1,0:T(8,128)S(1)} %get-tuple-element.39.g_ref), custom_call_target="tpu_custom_call" | custom-call | tf_op jit(solution)/shard_map/solve_last/pallas_call | solution.py:504
  207.9 28.4 %tail.1 = (bf16[512,256]{1,0:T(8,128)(2,1)S(1)}, f32[256,256]{1,0:T(8,128)S(1)}, f32[256,256]{1,0:T(8,128)S(1)}, bf16[512,256]{1,0:T(8,128)(2,1)S(1)}, f32[8,256...) custom-call(bf16[32,256]{1,0:T(8,128)(2,1)S(1)} %get-tuple-element.40.f_ref, f32[32,256]{1,0:T(8,128)S(1)} %get-tuple-element.37.w_ref, ...), custom_call_target="tpu_custom_call" | custom-call | tf_op jit(solution)/shard_map/tail/pallas_call | solution.py:596
  236.3 7.2 %fit.1 = (f32[256,256]{1,0:T(8,128)}, f32[512,256]{1,0:T(8,128)}, bf16[512,256]{1,0:T(8,128)(2,1)}, f32[1,1]{1,0:T(1,128)}, bf16[8,512,256]{2,1,0:T(8,128)(2,1)}) custom-call(f32[256,256]{1,0:T(8,128)S(1)} %get-tuple-element.44.lag_ref, f32[256,256]{1,0:T(8,128)S(1)} %get-tuple-element.45.base_ref, bf16[512,256]{1,0:T(8,128)(2,1)S(1)} %get-tuple-element.46.f_ref, ...), custom_call_target="tpu_custom_call" | custom-call | tf_op jit(solution)/shard_map/fit/pallas_call | solution.py:650
Async XLA Ops:
  0.6 1.0 copy-start

commit v4 on v3

--- a/solution.py
+++ b/solution.py
@@ -1,4 +1,5 @@
 import functools
+import math
 
 import jax
 import jax.numpy as jnp
@@ -115,6 +116,7 @@
         self.planes = lax.axis_size("series")
         self.times = lax.axis_size("tm")
         self.ring = self.times // 2
+        self.side = math.isqrt(self.planes)
         self.y = lax.div(self.t, 2)
         self.c = lax.rem(self.t, 2)
         self.partner = self.t + 1 - 2 * self.c
@@ -143,43 +145,61 @@
             meanwhile()
         pl.semaphore_wait(barrier, len(others))
 
+    def plane_at(self, k):
+        side = self.side
+        row = lax.rem(lax.div(self.p, side) + k // side, side)
+        return row * side + lax.rem(lax.rem(self.p, side) + k % side, side)
+
+    def plane_order(self):
+        def hops(k):
+            return sum(min(d, self.side - d) for d in divmod(k, self.side))
+
+        return sorted(range(1, self.planes), key=lambda k: -hops(k))
+
     def plane_others(self):
-        return [(lax.rem(self.p + k, self.planes), self.t) for k in range(1, self.planes)]
+        return [(self.plane_at(k), self.t) for k in self.plane_order()]
 
     def time_others(self):
         return [(self.p, lax.rem(self.t + k, self.times)) for k in range(1, self.times)]
 
     def share_plane(self, message, blocks, send, recv):
-        def start(k, carry):
-            to = lax.rem(self.p + k, self.planes)
+        for k in self.plane_order():
+            to = self.plane_at(k)
             self.copy(message, blocks.at[self.p], send.at[k], recv.at[self.p], p=to).start()
-            return carry
-
-        lax.fori_loop(1, self.planes, start, 0)
 
     def finish_plane(self, message, blocks, send, recv):
         def wait(k, carry):
-            other = lax.rem(self.p + k, self.planes)
+            other = self.plane_at(k)
             self.copy(message, blocks.at[other], send.at[k], recv.at[other], p=other).wait()
             return carry
 
         lax.fori_loop(1, self.planes, wait, 0)
 
     def spread_plane(self, pieces, blocks, send, recv):
-        def start(k, carry):
-            to = lax.rem(self.p + k, self.planes)
+        for k in self.plane_order():
+            to = self.plane_at(k)
             self.copy(pieces.at[to], blocks.at[self.p], send.at[k], recv.at[self.p], p=to).start()
-            return carry
-
-        lax.fori_loop(1, self.planes, start, 0)
 
     def finish_spread(self, pieces, blocks, send, recv):
         def wait(k, carry):
-            other = lax.rem(self.p + k, self.planes)
+            other = self.plane_at(k)
             self.copy(pieces.at[other], blocks.at[other], send.at[k], recv.at[other], p=other).wait()
             return carry
 
         lax.fori_loop(1, self.planes, wait, 0)
+
+    def split_times(self, pieces, blocks, send, recv):
+        def start(k, carry):
+            to = lax.rem(self.t + k, self.times)
+            piece = pieces.at[lax.rem(to, 2)]
+            self.copy(piece, blocks.at[self.t], send.at[k], recv.at[self.t], t=to).start()
+            return carry
+
+        lax.fori_loop(1, self.times, start, 0)
+
+    def swap(self, halves, send, recv):
+        mine = halves.at[self.c]
+        return self.copy(mine, mine, send, recv, t=self.partner)
 
     def share_times(self, message, blocks, send, recv):
         def start(k, carry):
@@ -216,18 +236,23 @@
         taken, refs[:] = refs[:count], refs[count:]
         return taken
 
-    x_ref, f_ref, w_ref, m_ref, g_ref = take(5)
+    if first:
+        x_ref, f_ref = take(2)
+    else:
+        x_ref, before_ref, inverse_ref, ridged_ref = take(4)
+    w_ref, n_ref, g_ref = take(3)
     if last:
-        all_ref, square_ref = take(2)
+        m_ref, all_ref, square_ref = take(3)
     if first:
         x_from = x_ref
         x_ref, x_sem = take(2)
     else:
-        fbuf, f_s, f_r = take(3)
+        f_ref, fbuf, f_s, f_r = take(4)
     part, other, chip, acc, relay_in, direct_in, relay_out, joined_in = take(8)
     gram, gram_in, gram_all, moment, moment_in, moment_own, moment_times, moment_all = take(8)
     pbuf, wacc, winc = take(3)
     pair_s, pair_r, ring_s, ring_r, ga_s, ga_r, gb_s, gb_r = take(8)
+    moment_full, swap_s, swap_r = take(3)
     gpair_s, gpair_r, gring_s, gring_r, ma_s, ma_r, mb_s, mb_r, mc_s, mc_r, w_s, w_r = take(12)
     me = Place()
     rows = acc.shape[1]
@@ -244,7 +269,10 @@
         gram[...] = column_gram(f_ref[...], f_ref[...])
         x_copy.wait()
 
-    me.greet(me.time_others() + me.plane_others(), bring if first else None)
+    def solved():
+        f_ref[...] = next_factors(before_ref, inverse_ref[...], ridged_ref[...])
+
+    me.greet(me.time_others() + me.plane_others(), bring if first else solved)
 
     if first:
         def factors():
@@ -375,9 +403,9 @@
     far_down.start()
 
     me.finish_spread(moment, moment_in, ma_s, ma_r)
-    moment_own[...] = total_of(moment_in)
-    me.share_times(moment_own, moment_times, mb_s, mb_r)
-    moment_times[me.t] = moment_own[...]
+    moment_own[...] = total_of(moment_in).reshape(moment_own.shape)
+    me.split_times(moment_own, moment_times, mb_s, mb_r)
+    moment_times[me.t] = moment_own[me.c]
 
     up_high.wait_recv()
     pass_over(down).start()
@@ -387,9 +415,10 @@
     contribute(t_up)
     across(down)
     across(up)
-    me.finish_times(moment_own, moment_times, mb_s, mb_r)
-    moment_all[me.p] = total_of(moment_times)
-    me.share_plane(moment_all.at[me.p], moment_all, mc_s, mc_r)
+    me.finish_times(moment_own.at[0], moment_times, mb_s, mb_r)
+    moment_all[me.c, me.p] = total_of(moment_times)
+    moment_mine = moment_all.at[me.c]
+    me.share_plane(moment_mine.at[me.p], moment_mine, mc_s, mc_r)
     far_up.wait_recv()
     far_down.wait_recv()
     pass_over(far).start()
@@ -401,11 +430,20 @@
     if last:
         all_ref[...] = pbuf[...]
     me.finish_plane(gram_all.at[me.p], gram_all, gb_s, gb_r)
-    g_ref[...] = gram_all[...].reshape(g_ref.shape)
-    me.finish_plane(moment_all.at[me.p], moment_all, mc_s, mc_r)
-    m_ref[...] = moment_all[...].reshape(m_ref.shape)
+    g_ref[...] = regularized(gram_all[...].reshape(g_ref.shape))
+    n_ref[...] = RIDGE * wide(g_ref[...], g_ref[...])
+    me.finish_plane(moment_mine.at[me.p], moment_mine, mc_s, mc_r)
+    swap = me.swap(moment_all, swap_s, swap_r)
+    swap.start()
     me.finish_spread(wacc, winc, w_s, w_r)
     w_ref[...] = total_of(winc)
+    swap.wait()
+    for core in range(2):
+        moment_full[:, core] = moment_all[core]
+    total = moment_full[...].reshape(n_ref.shape)
+    n_ref[...] += total
+    if last:
+        m_ref[...] = total
 
     for sent in (relay_up, relay_down, direct_up, direct_down, joined_up, joined_down):
         sent.wait_send()
@@ -416,10 +454,10 @@
         pass_over(y).wait_send()
 
 
-def sweep(data, factors, first, last):
+def sweep(data, held, first, last):
     planes, times = lax.axis_size("series"), lax.axis_size("tm")
     ring = times // 2
-    n = factors.shape[1]
+    n = held[0].shape[1]
     span = data.shape[1]
     rows = data.shape[0] // times
     half = rows // 2
@@ -431,6 +469,7 @@
     ]
     if last:
         out_shape += [
+            jax.ShapeDtypeStruct((n, n), F32),
             jax.ShapeDtypeStruct((times, rows, n), BF16),
             jax.ShapeDtypeStruct((8, n), F32),
         ]
@@ -439,7 +478,8 @@
         out_shape += [jax.ShapeDtypeStruct(data.shape, BF16)]
         scratch += [DMA]
     else:
-        scratch += [pltpu.VMEM((planes, tall, n), BF16), DMA((planes,)), DMA((planes,))]
+        scratch += [pltpu.VMEM((tall, n), BF16), pltpu.VMEM((planes, tall, n), BF16)]
+        scratch += [DMA((planes,)), DMA((planes,))]
     scratch += [pltpu.VMEM((ring, rows, n), BF16)] * 3 + [pltpu.VMEM((ring, rows, n), F32)]
     scratch += [pltpu.VMEM((2, half, n), BF16)] * 4
     scratch += [
@@ -448,22 +488,25 @@
         pltpu.VMEM((planes, slab, n), F32),
         pltpu.VMEM((planes, slab, n), F32),
         pltpu.VMEM((planes, slab, n), F32),
-        pltpu.VMEM((slab, n), F32),
-        pltpu.VMEM((times, slab, n), F32),
-        pltpu.VMEM((planes, slab, n), F32),
+        pltpu.VMEM((2, slab // 2, n), F32),
+        pltpu.VMEM((times, slab // 2, n), F32),
+        pltpu.VMEM((2, planes, slab // 2, n), F32),
         pltpu.VMEM((times, rows, n), BF16),
         pltpu.VMEM((planes, tall, n), F32),
         pltpu.VMEM((planes, tall, n), F32),
     ]
     scratch += [DMA((ring,)), DMA((ring,)), DMA((6,)), DMA((6,))]
     scratch += [DMA((times,)), DMA((times,)), DMA((planes,)), DMA((planes,))]
+    scratch += [pltpu.VMEM((planes, 2, slab // 2, n), F32), DMA, DMA]
     scratch += [DMA((ring,)), DMA((ring,)), DMA((6,)), DMA((6,))]
     scratch += [DMA((planes,)), DMA((planes,)), DMA((times,)), DMA((times,))]
     scratch += [DMA((planes,)), DMA((planes,)), DMA((planes,)), DMA((planes,))]
     return pl.pallas_call(
         functools.partial(sweep_kernel, first, last),
         out_shape=tuple(out_shape),
-        in_specs=[pl.BlockSpec(memory_space=pltpu.HBM if first else pltpu.VMEM), *in_vmem(1)],
+        in_specs=[
+            pl.BlockSpec(memory_space=pltpu.HBM if first else pltpu.VMEM), *in_vmem(len(held))
+        ],
         out_specs=tuple(in_vmem(len(out_shape))),
         scratch_shapes=scratch,
         compiler_params=pltpu.CompilerParams(
@@ -472,7 +515,7 @@
             vmem_limit_bytes=(48 if first else 32) * 1024 * 1024,
         ),
         name="sweep_first" if first else "sweep_last" if last else "sweep",
-    )(data, factors)
+    )(data, *held)
 
 
 def regularized(gram):
@@ -485,31 +528,24 @@
     return wide(wide(w_ref[...], inverse), ridged).astype(BF16)
 
 
-def solve_kernel(w_ref, m_ref, g_ref, f_ref, *state):
-    ridged = regularized(g_ref[...])
-    (inverse,) = inverses_of([m_ref[...] + RIDGE * wide(ridged, ridged)], *state)
-    f_ref[...] = next_factors(w_ref, inverse, ridged)
-
-
-def solve_last_kernel(w_ref, m_ref, g_ref, f_ref, inverse_ref, *state):
-    ridged = regularized(g_ref[...])
-    combined = m_ref[...] + RIDGE * wide(ridged, ridged)
-    inverse, inverse_ref[...] = inverses_of([combined, ridged], *state)
-    f_ref[...] = next_factors(w_ref, inverse, ridged)
-
-
-def solve(cross, moment, gram, last):
-    factors = jax.ShapeDtypeStruct(cross.shape, BF16)
-    square = jax.ShapeDtypeStruct(gram.shape, F32)
+def solve_kernel(count, *refs):
+    grams, inverses, state = refs[:count], refs[count : 2 * count], refs[2 * count :]
+    for ref, inverse in zip(inverses, inverses_of([g[...] for g in grams], *state)):
+        ref[...] = inverse
+
+
+def solve(*grams):
+    count = len(grams)
+    square = jax.ShapeDtypeStruct(grams[0].shape, F32)
     return pl.pallas_call(
-        solve_last_kernel if last else solve_kernel,
-        out_shape=(factors, square) if last else (factors,),
-        in_specs=in_vmem(3),
-        out_specs=tuple(in_vmem(2 if last else 1)),
-        scratch_shapes=squares_of(2 if last else 1, gram.shape[0]),
+        functools.partial(solve_kernel, count),
+        out_shape=(square,) * count,
+        in_specs=in_vmem(count),
+        out_specs=tuple(in_vmem(count)),
+        scratch_shapes=squares_of(count, square.shape[0]),
         compiler_params=pltpu.CompilerParams(vmem_limit_bytes=16 * 1024 * 1024),
-        name="solve_last" if last else "solve",
-    )(cross, moment, gram)
+        name="solve" if count == 1 else "solve_both",
+    )(*grams)
 
 
 def folded(rows):
@@ -519,27 +555,35 @@
 
 
 def tail_kernel(
-    f_ref, w_ref, m_ref, inverse_ref, p_ref, square_ref,
+    w_ref, combined_ref, ridged_ref, m_ref, inverse_ref, p_ref, square_ref,
     all_ref, lag_ref, base_ref, earlier_ref, sums_ref, l_ref,
-    top, middle, bottom, fbuf, before, lag, base, message, message_in, message_all,
-    f_s, f_r, row_s, row_r, ta_s, ta_r, tb_s, tb_r,
+    f_ref, top, middle, bottom, fbuf, before, lag, base, message, message_in, message_all, whole,
+    f_s, f_r, row_s, row_r, ta_s, ta_r, tb_s, tb_r, swap_s, swap_r,
 ):
     me = Place()
     span, n = all_ref.shape
     edge = before.shape[0]
-    me.greet(me.time_others() + me.plane_others())
+
+    def solved():
+        f_ref[...] = next_factors(w_ref, combined_ref[...], ridged_ref[...])
+
+    me.greet(me.time_others() + me.plane_others(), solved)
     me.share_plane(f_ref, fbuf, f_s, f_r)
     fbuf[me.p] = f_ref[...]
     slab = n // me.planes
+    part = slab // 2
 
     inverse = inverse_ref[...]
     known = f_ref[...].astype(F32)
     quadratic = wide(wide(inverse, m_ref[...]), inverse)
     side = n // 2
-    message[2 * slab :, :side] = folded(wide(known, quadratic) * known) - 2.0 * folded(
+    terms = folded(wide(known, quadratic) * known) - 2.0 * folded(
         wide(known, inverse) * w_ref[...]
     )
-    message[2 * slab :, side:] = folded(square_ref[...])
+    squared = folded(square_ref[...])
+    for core in range(2):
+        message[core, slab:, :side] = terms
+        message[core, slab:, side:] = squared
     top[...] = inverse.astype(BF16)
     rest = inverse - top[...].astype(F32)
     middle[...] = rest.astype(BF16)
@@ -569,27 +613,35 @@
     earlier_ref[...] = earlier
     lag[...] = column_gram(factors, earlier)
     base[...] = column_gram(earlier, earlier)
-    here = pl.ds(pl.multiple_of(me.p * slab, slab), slab)
-    message[:slab, :] = lag[here, :]
-    message[slab : 2 * slab, :] = base[here, :]
-    me.share_times(message, message_in, ta_s, ta_r)
-    message_in[me.t] = message[...]
+    for core in range(2):
+        here = pl.ds(pl.multiple_of(me.p * slab + core * part, part), part)
+        message[core, :part, :] = lag[here, :]
+        message[core, part:slab, :] = base[here, :]
+    me.split_times(message, message_in, ta_s, ta_r)
+    message_in[me.t] = message[me.c]
     lax.fori_loop(count // 4, count // 2, load, 0)
-    me.finish_times(message, message_in, ta_s, ta_r)
-    message_all[me.p] = total_of(message_in)
-    me.share_plane(message_all.at[me.p], message_all, tb_s, tb_r)
+    me.finish_times(message.at[0], message_in, ta_s, ta_r)
+    message_all[me.c, me.p] = total_of(message_in)
+    message_mine = message_all.at[me.c]
+    me.share_plane(message_mine.at[me.p], message_mine, tb_s, tb_r)
     lax.fori_loop(count // 2, count, load, 0)
-    me.finish_plane(message_all.at[me.p], message_all, tb_s, tb_r)
-    lag_ref[...] = message_all[:, :slab, :].reshape(n, n)
-    base_ref[...] = message_all[:, slab : 2 * slab, :].reshape(n, n)
-    sums_ref[...] = total_of(message_all[:, 2 * slab :, :])
-
-
-def tail(factors, cross, moment, inverse, projection, squares):
+    me.finish_plane(message_mine.at[me.p], message_mine, tb_s, tb_r)
+    swap = me.swap(message_all, swap_s, swap_r)
+    swap.start()
+    swap.wait()
+    for core in range(2):
+        whole[0, :, core] = message_all[core, :, :part, :]
+        whole[1, :, core] = message_all[core, :, part:slab, :]
+    lag_ref[...] = whole[0].reshape(n, n)
+    base_ref[...] = whole[1].reshape(n, n)
+    sums_ref[...] = total_of(message_all[0, :, slab:, :])
+
+
+def tail(cross, combined, ridged, moment, inverse, projection, squares):
     planes, times = lax.axis_size("series"), lax.axis_size("tm")
-    slab, n = factors.shape
+    slab, n = cross.shape
     span = slab * planes
-    tall = 2 * (n // planes) + squares.shape[0]
+    tall = n // planes + squares.shape[0]
     square = jax.ShapeDtypeStruct((n, n), F32)
     block = jax.ShapeDtypeStruct((span, n), BF16)
     sums = jax.ShapeDtypeStruct(squares.shape, F32)
@@ -598,9 +650,10 @@
         out_shape=(
             block, square, square, block, sums, jax.ShapeDtypeStruct(projection.shape, BF16)
         ),
-        in_specs=in_vmem(6),
+        in_specs=in_vmem(7),
         out_specs=tuple(in_vmem(6)),
         scratch_shapes=[
+            pltpu.VMEM((slab, n), BF16),
             pltpu.VMEM((n, n), BF16),
             pltpu.VMEM((n, n), BF16),
             pltpu.VMEM((n, n), BF16),
@@ -608,17 +661,18 @@
             pltpu.VMEM((16, n), BF16),
             pltpu.VMEM((n, n), F32),
             pltpu.VMEM((n, n), F32),
-            pltpu.VMEM((tall, n), F32),
+            pltpu.VMEM((2, tall, n), F32),
             pltpu.VMEM((times, tall, n), F32),
-            pltpu.VMEM((planes, tall, n), F32),
+            pltpu.VMEM((2, planes, tall, n), F32),
+            pltpu.VMEM((2, planes, 2, n // planes // 2, n), F32),
             DMA((planes,)), DMA((planes,)), DMA, DMA,
-            DMA((times,)), DMA((times,)), DMA((planes,)), DMA((planes,)),
+            DMA((times,)), DMA((times,)), DMA((planes,)), DMA((planes,)), DMA, DMA,
         ],
         compiler_params=pltpu.CompilerParams(
             collective_id=3, has_side_effects=True, vmem_limit_bytes=32 * 1024 * 1024
         ),
         name="tail",
-    )(factors, cross, moment, inverse, projection, squares)
+    )(cross, combined, ridged, moment, inverse, projection, squares)
 
 
 def fit_kernel(
@@ -669,16 +723,18 @@
 
 
 def body(data, factors_init):
-    factors, held = factors_init, data
+    held, here = (factors_init,), data
     for step in range(ITERS):
         first, last = step == 0, step == ITERS - 1
-        cross, moment, gram, *extra = sweep(held, factors, first, last)
+        cross, combined, ridged, *extra = sweep(here, held, first, last)
         if first:
-            (held,) = extra
-        factors, *inverse = solve(cross, moment, gram, last)
-    projection, squares = extra
+            (here,) = extra
+        if not last:
+            held = (cross, *solve(combined), ridged)
+    moment, projection, squares = extra
+    combined, inverse = solve(combined, ridged)
     gathered, lagged, base, earlier, sums, loadings = tail(
-        factors, cross, moment, *inverse, projection, squares
+        cross, combined, ridged, moment, inverse, projection, squares
     )
     transition, innovations, factors, share, loadings = fit(
         lagged, base, gathered, earlier, sums, loadings

time: 245 us -> 235 us (0.959)
  Pallas kernels: 242 us -> 231 us
    pallas_call x3, Pallas kernels: 145 us -> 138 us  [sweep(): pl.pallas_call(functools.partial(sweep_kernel, first, last), out_shape=tu...]
    pallas_call x1, Pallas kernels: 28.4 us -> 25.4 us  [tail(): pl.pallas_call(tail_kernel, out_shape=(block, square, square, block, sums...]
where the time goes in v4:
time: 235 us; the launch traced here: 233 us
  Pallas kernels  231 us (98%)
    pallas_call x3, Pallas kernels, sweep(): pl.pallas_call(functools.partial(sweep_kernel, first, last), out_shape=tu...  138 us
    pallas_call x3, Pallas kernels, solve(): pl.pallas_call(functools.partial(solve_kernel, count), out_shape=(square,...  60.5 us
    pallas_call x1, Pallas kernels, tail(): pl.pallas_call(tail_kernel, out_shape=(block, square, square, block, sums...  25.4 us
    pallas_call x1, Pallas kernels, fit(): pl.pallas_call(fit_kernel, out_shape=(jax.ShapeDtypeStruct((n, n), F32),...  6.65 us

profile of v4, /device:TPU:1, one launch (start us, length us, event | category | flops | bytes accessed | tf_op | source)
XLA Modules:
  0.0 232.8 jit_solution(14984219245715328991)
XLA Ops:
  0.6 0.0 copy-start
  0.6 0.9 copy-done
  1.6 44.5 %sweep_first.1 = (f32[32,256]{1,0:T(8,128)S(1)}, f32[256,256]{1,0:T(8,128)S(1)}, f32[256,256]{1,0:T(8,128)S(1)}, bf16[4096,512]{1,0:T(8,128)(2,1)S(1)}) custom-call(bf16[4096,512]{1,0:T(8,128)(2,1)} %refs_0_.1, bf16[512,256]{1,0:T(8,128)(2,1)S(1)} %copy-done), custom_call_target="tpu_custom_call" | custom-call | tf_op jit(solution)/shard_map/sweep_first/pallas_call | solution.py:504
  46.1 5.7 %solve.2.refs_2_ = f32[256,256]{1,0:T(8,128)S(1)} custom-call(f32[256,256]{1,0:T(8,128)S(1)} %get-tuple-element.33.refs_0_), custom_call_target="tpu_custom_call" | custom-call | tf_op jit(solution)/shard_map/solve/pallas_call | solution.py:540
  51.9 47.2 %sweep.1 = (f32[32,256]{1,0:T(8,128)S(1)}, f32[256,256]{1,0:T(8,128)S(1)}, f32[256,256]{1,0:T(8,128)S(1)}) custom-call(bf16[4096,512]{1,0:T(8,128)(2,1)S(1)} %get-tuple-element.31.refs_0_, f32[32,256]{1,0:T(8,128)S(1)} %get-tuple-element.32.refs_1_, f32[256,256]{1,0:T(8,128)S(1)} %solve.2.refs_2_, f32[256,256]{1,0:T(8,128)S(1)} %get-tuple-element.34.refs_3_), custom_call_target="tpu_custom_call" | custom-call | tf_op jit(solution)/shard_map/sweep/pallas_call | solution.py:504
  99.0 25.2 %solve.3.refs_2_ = f32[256,256]{1,0:T(8,128)S(1)} custom-call(f32[256,256]{1,0:T(8,128)S(1)} %get-tuple-element.36.refs_0_), custom_call_target="tpu_custom_call" | custom-call | tf_op jit(solution)/shard_map/solve/pallas_call | solution.py:540
  124.2 46.7 %sweep_last.1 = (f32[32,256]{1,0:T(8,128)S(1)}, f32[256,256]{1,0:T(8,128)S(1)}, f32[256,256]{1,0:T(8,128)S(1)}, f32[256,256]{1,0:T(8,128)S(1)}, bf16[8,512,256]{2,1,0:T(8,128)(2,1)S(1)}, /*index=5*/f32[8,256]{1,0:T(8,128)S(1)}) custom-call(bf16[4096,512]{1,0:T(8,128)(2,1)S(1)} %get-tuple-element.31.refs_0_, f32[32,256]{1,0:T(8,128)S(1)} %get-tuple-element.35.refs_1_, ...), custom_call_target="tpu_custom_call" | custom-call | tf_op jit(solution)/shard_map/sweep_last/pallas_call | solution.py:504
  170.9 29.6 %solve_both.1 = (f32[256,256]{1,0:T(8,128)S(1)}, f32[256,256]{1,0:T(8,128)S(1)}) custom-call(f32[256,256]{1,0:T(8,128)S(1)} %get-tuple-element.39.refs_0_, f32[256,256]{1,0:T(8,128)S(1)} %get-tuple-element.40.refs_1_.ridged_ref), custom_call_target="tpu_custom_call" | custom-call | tf_op jit(solution)/shard_map/solve_both/pallas_call | solution.py:540
  200.5 25.4 %tail.1 = (bf16[512,256]{1,0:T(8,128)(2,1)S(1)}, f32[256,256]{1,0:T(8,128)S(1)}, f32[256,256]{1,0:T(8,128)S(1)}, bf16[512,256]{1,0:T(8,128)(2,1)S(1)}, f32[8,256...) custom-call(f32[32,256]{1,0:T(8,128)S(1)} %get-tuple-element.38.w_ref, f32[256,256]{1,0:T(8,128)S(1)} %get-tuple-element.41.combined_ref, ...), custom_call_target="tpu_custom_call" | custom-call | tf_op jit(solution)/shard_map/tail/pallas_call | solution.py:648
  225.9 6.7 %fit.1 = (f32[256,256]{1,0:T(8,128)}, f32[512,256]{1,0:T(8,128)}, bf16[512,256]{1,0:T(8,128)(2,1)}, f32[1,1]{1,0:T(1,128)}, bf16[8,512,256]{2,1,0:T(8,128)(2,1)}) custom-call(f32[256,256]{1,0:T(8,128)S(1)} %get-tuple-element.46.lag_ref, f32[256,256]{1,0:T(8,128)S(1)} %get-tuple-element.47.base_ref, bf16[512,256]{1,0:T(8,128)(2,1)S(1)} %get-tuple-element.48.f_ref, ...), custom_call_target="tpu_custom_call" | custom-call | tf_op jit(solution)/shard_map/fit/pallas_call | solution.py:704
Async XLA Ops:
  0.6 1.0 copy-start
